TPU v7x, 32 devices: a whole 2x2x4 slice. The times are simulated.
32 devices in a mesh: hp: 4 (over x, y), cp: 8 (over z, core).
Axes of the slice: x: 2, y: 2, z: 4, core: 2. Of those that a mesh axis runs over, the one named last changes fastest.
Arguments:
- q: bfloat16 [6144, 12, 128], P('cp', 'hp'), parts along dimension 1
- k: bfloat16 [6144, 12, 128], P('cp', 'hp'), parts along dimension 1
- v: bfloat16 [6144, 12, 128], P('cp', 'hp'), parts along dimension 1
- u_bias: float32 [12, 128], P('hp'), parts along dimension 0
- v_bias: float32 [12, 128], P('hp'), parts along dimension 0
- rel_table: bfloat16 [6144, 1536], P('cp')
- w_rel: bfloat16 [1536, 12, 128], P(None, 'hp'), parts along dimension 1
- d_out: bfloat16 [6144, 12, 128], P('cp', 'hp'), parts along dimension 1
Outputs:
- output 1: bfloat16 [6144, 12, 128], P('cp', 'hp'), parts along dimension 1
- output 2: bfloat16 [6144, 12, 128], P('cp', 'hp'), parts along dimension 1
- output 3: bfloat16 [6144, 12, 128], P('cp', 'hp'), parts along dimension 1
- output 4: bfloat16 [6144, 12, 128], P('cp', 'hp'), parts along dimension 1
- output 5: float32 [12, 128], P('hp'), parts along dimension 0
- output 6: float32 [12, 128], P('hp'), parts along dimension 0
- output 7: float32 [1536, 12, 128], P(None, 'hp'), parts along dimension 1
There are 4 independent parts. A program takes and returns all parts, laid end to end along the dimension named above; an argument that names none is the same for every part.
All inputs are finite; a program needn't handle non-finite values.
Results may differ from a plain program's by a relative error of at most 0.014711.
Values are sent between devices in bfloat16 or wider.
A program may use at most 1 GiB of HBM per device.

v0:
```python
import jax
import jax.numpy as jnp
from jax import lax
from jax.sharding import PartitionSpec as P


def skew_scores(by_offset):
    lead_dims = by_offset.shape[:-2]
    block_len = by_offset.shape[-2]
    flat_view = by_offset.reshape(lead_dims + (2 * block_len * block_len,))
    kept_view = flat_view[..., block_len - 1:block_len - 1 + block_len * (2 * block_len - 1)]
    return kept_view.reshape(lead_dims + (block_len, 2 * block_len - 1))[..., :block_len]


def unskew_scores(by_key):
    lead_dims = by_key.shape[:-2]
    block_len = by_key.shape[-1]
    pad_lead = [(0, 0)] * len(lead_dims)
    widened = jnp.pad(by_key, pad_lead + [(0, 0), (0, block_len - 1)])
    flat_view = widened.reshape(lead_dims + (block_len * (2 * block_len - 1),))
    flat_view = jnp.pad(flat_view, pad_lead + [(block_len - 1, 1)])
    return flat_view.reshape(lead_dims + (block_len, 2 * block_len))


def solution(mesh):
    n_dev = mesh.shape['cp']
    shift_pairs = [(src_dev, (src_dev + 1) % n_dev) for src_dev in range(n_dev)]
    last_step = n_dev - 1
    seq_spec = P('cp', 'hp', None)
    head_spec = P('hp', None)
    weight_spec = P(None, 'hp', None)

    def local_fn(q, k, v, u_bias, v_bias, rel_table, w_rel, d_out):
        block_len, num_heads, head_dim = q.shape
        inv_sqrt = head_dim ** -0.5
        my_block = lax.axis_index('cp')
        rel_mine = jnp.einsum('uo,ojf->ujf', rel_table, w_rel, preferred_element_type=jnp.float32).astype(jnp.bfloat16)
        rel_flipped = lax.all_gather(rel_mine[::-1], 'cp')
        q_wide = q.astype(jnp.float32)
        q_u = (q_wide + u_bias).astype(jnp.bfloat16)
        q_v = (q_wide + v_bias).astype(jnp.bfloat16)
        row_ids = jnp.arange(block_len)
        above_diag = row_ids[None, :] > row_ids[:, None]

        def rel_window(distance):
            near_blk = lax.dynamic_index_in_dim(rel_flipped, distance, 0, keepdims=False)
            far_blk = lax.dynamic_index_in_dim(rel_flipped, jnp.maximum(distance - 1, 0), 0, keepdims=False)
            return jnp.concatenate([near_blk, far_blk], axis=0)

        def block_scores(k_blk, window, distance):
            content = jnp.einsum('qhd,khd->hqk', q_u, k_blk, preferred_element_type=jnp.float32)
            by_offset = jnp.einsum('qhd,shd->hqs', q_v, window, preferred_element_type=jnp.float32)
            score_ij = (content + skew_scores(by_offset)) * inv_sqrt
            return jnp.where(above_diag & (distance == 0), -jnp.inf, score_ij)

        def attend(distance, k_blk, v_blk, run_stats):
            run_max, run_sum, out_acc = run_stats
            score_ij = block_scores(k_blk, rel_window(distance), distance)
            new_max = jnp.maximum(run_max, score_ij.max(axis=-1))
            prob_ij = jnp.exp(score_ij - new_max[..., None])
            rescale = jnp.exp(run_max - new_max)
            run_sum = rescale * run_sum + prob_ij.sum(axis=-1)
            out_acc = out_acc * rescale.T[:, :, None] + jnp.einsum('hqk,khd->qhd', prob_ij.astype(jnp.bfloat16), v_blk, preferred_element_type=jnp.float32)
            return new_max, run_sum, out_acc

        def fwd_step(step_idx, carry):
            k_blk, v_blk, run_stats = carry
            run_stats = lax.cond(step_idx <= my_block, lambda stats_in: attend(step_idx, k_blk, v_blk, stats_in), lambda stats_in: stats_in, run_stats)
            k_blk = lax.ppermute(k_blk, 'cp', shift_pairs)
            v_blk = lax.ppermute(v_blk, 'cp', shift_pairs)
            return k_blk, v_blk, run_stats

        run_stats = (
            jnp.full((num_heads, block_len), -jnp.inf, jnp.float32),
            jnp.zeros((num_heads, block_len), jnp.float32),
            jnp.zeros((block_len, num_heads, head_dim), jnp.float32),
        )
        k_blk, v_blk, run_stats = lax.fori_loop(0, last_step, fwd_step, (k, v, run_stats))
        run_stats = lax.cond(last_step <= my_block, lambda stats_in: attend(last_step, k_blk, v_blk, stats_in), lambda stats_in: stats_in, run_stats)
        run_max, run_sum, out_acc = run_stats
        out_full = out_acc / run_sum.T[:, :, None]
        log_norm = run_max + jnp.log(run_sum)
        row_delta = jnp.sum(d_out.astype(jnp.float32) * out_full, axis=-1).T

        def grad_block(distance, k_blk, v_blk, grad_state):
            dk_acc, dv_acc, grad_qu, grad_qv, grad_rel = grad_state
            window = rel_window(distance)
            score_ij = block_scores(k_blk, window, distance)
            prob_ij = jnp.exp(score_ij - log_norm[..., None])
            d_prob = jnp.einsum('qhd,khd->hqk', d_out, v_blk, preferred_element_type=jnp.float32)
            d_score = (prob_ij * (d_prob - row_delta[..., None]) * inv_sqrt).astype(jnp.bfloat16)
            dv_acc = dv_acc + jnp.einsum('hqk,qhd->khd', prob_ij.astype(jnp.bfloat16), d_out, preferred_element_type=jnp.float32)
            dk_acc = dk_acc + jnp.einsum('hqk,qhd->khd', d_score, q_u, preferred_element_type=jnp.float32)
            grad_qu = grad_qu + jnp.einsum('hqk,khd->qhd', d_score, k_blk, preferred_element_type=jnp.float32)
            d_wide = unskew_scores(d_score)
            grad_qv = grad_qv + jnp.einsum('hqs,shd->qhd', d_wide, window, preferred_element_type=jnp.float32)
            d_window = jnp.einsum('hqs,qhd->shd', d_wide, q_v, preferred_element_type=jnp.float32)
            near_sum = lax.dynamic_index_in_dim(grad_rel, distance, 0, keepdims=False) + d_window[:block_len]
            grad_rel = lax.dynamic_update_index_in_dim(grad_rel, near_sum, distance, 0)
            far_idx = jnp.maximum(distance - 1, 0)
            far_sum = lax.dynamic_index_in_dim(grad_rel, far_idx, 0, keepdims=False) + d_window[block_len:]
            grad_rel = lax.dynamic_update_index_in_dim(grad_rel, far_sum, far_idx, 0)
            return dk_acc, dv_acc, grad_qu, grad_qv, grad_rel

        def bwd_step(step_idx, carry):
            k_blk, v_blk, grad_state = carry
            grad_state = lax.cond(step_idx <= my_block, lambda grads_in: grad_block(step_idx, k_blk, v_blk, grads_in), lambda grads_in: grads_in, grad_state)
            dk_acc, dv_acc, grad_qu, grad_qv, grad_rel = grad_state
            k_blk = lax.ppermute(k_blk, 'cp', shift_pairs)
            v_blk = lax.ppermute(v_blk, 'cp', shift_pairs)
            dk_acc = lax.ppermute(dk_acc, 'cp', shift_pairs)
            dv_acc = lax.ppermute(dv_acc, 'cp', shift_pairs)
            return k_blk, v_blk, (dk_acc, dv_acc, grad_qu, grad_qv, grad_rel)

        blk_zeros = jnp.zeros((block_len, num_heads, head_dim), jnp.float32)
        grad_state = (blk_zeros, blk_zeros, blk_zeros, blk_zeros, jnp.zeros((n_dev, block_len, num_heads, head_dim), jnp.float32))
        k_blk, v_blk, grad_state = lax.fori_loop(0, last_step, bwd_step, (k, v, grad_state))
        grad_state = lax.cond(last_step <= my_block, lambda grads_in: grad_block(last_step, k_blk, v_blk, grads_in), lambda grads_in: grads_in, grad_state)
        dk_acc, dv_acc, grad_qu, grad_qv, grad_rel = grad_state
        dk_acc = lax.ppermute(dk_acc, 'cp', shift_pairs)
        dv_acc = lax.ppermute(dv_acc, 'cp', shift_pairs)
        rel_grad_mine = lax.psum_scatter(grad_rel, 'cp', scatter_dimension=0, tiled=False)
        d_rel = rel_grad_mine[::-1].astype(jnp.bfloat16)
        d_w_rel = lax.psum(jnp.einsum('uo,ujf->ojf', rel_table, d_rel, preferred_element_type=jnp.float32), 'cp')
        d_u_bias = lax.psum(grad_qu.sum(axis=0), 'cp')
        d_v_bias = lax.psum(grad_qv.sum(axis=0), 'cp')
        return (
            out_full.astype(jnp.bfloat16),
            (grad_qu + grad_qv).astype(jnp.bfloat16),
            dk_acc.astype(jnp.bfloat16),
            dv_acc.astype(jnp.bfloat16),
            d_u_bias,
            d_v_bias,
            d_w_rel,
        )

    return jax.shard_map(
        local_fn,
        mesh=mesh,
        in_specs=(seq_spec, seq_spec, seq_spec, head_spec, head_spec, P('cp', None), weight_spec, seq_spec),
        out_specs=(seq_spec, seq_spec, seq_spec, seq_spec, head_spec, head_spec, weight_spec),
        check_vma=False,
    )
```

profile of v0, /device:TPU:0, one launch (start us, length us, event | category | flops | bytes accessed | tf_op | source)
XLA Modules:
  0.0 3352.0 jit_solution(17493054542314955182)
XLA Ops:
  23.6 48.6 %all-gather.3.cloned.1.call-done = bf16[6144,3,128]{2,0,1:T(8,128)(2,1)} async-done(((bf16[768,3,128]{2,0,1:T(8,128)(2,1)}), bf16[6144,3,128]{2,0,1:T(8,128)(2,1)}) %all-gather.3.cloned.1.call-update) | async-done | bytes 4718608 | tf_op jit(solution)/shard_map/all_gather | solution.py:38
  78.8 939.9 %while.48 = (s32[]{:T(128)}, bf16[768,3,128]{2,0,1:T(8,128)(2,1)}, bf16[768,3,128]{2,0,1:T(8,128)(2,1)}, f32[3,768]{1,0:T(4,128)S(1)}, f32[3,768]{1,0:T(4,128)},...) while((s32[]{:T(128)}, bf16[768,3,128]{2,0,1:T(8,128)(2,1)}, ...), condition=%wide.region_5.6_spmd.clone, body=%wide.region_0.5_spmd.clone.sunk | while | flops 1830230784 | bytes 247892528 | solution.py:78
  86.3 145.4 %conditional.10 = ((f32[3,768]{1,0:T(4,128)S(1)}, f32[3,768]{1,0:T(4,128)}, f32[768,3,128]{2,0,1:T(8,128)})) conditional(s32[]{:T(128)} %convert_element_type.128, (f32[3,768]{1,0:T(4,128)S(1)}, f32[3,768]{1,0:T(4,128)}, f32[768,3,128]{2,0,1:T(8,128)}) %tuple.140, (s32[]{:T(128)}, s32[768,768]{0,1:T(8,128)}, bf16[768,3,128]{2,0,1:T(8,128)(2,1)S(1)}, ...), branch_computations={%region_1.0_spmd, %region_2.4_spmd} | conditional | flops 1830230784 | bytes 236095712 | solution.py:68
  87.6 7.0 convolution_bitcast_fusion
  94.6 15.1 copy.33
  109.8 18.7 copy.73
  128.5 12.4 slice.44
  140.9 40.8 %reshape.65 = f32[3536640]{0:T(1024)} reshape(f32[3,1178880]{1,0:T(4,128)} %slice.44) | data formatting | bytes 28293120 | tf_op jit(solution)/shard_map/while/body/eval_jaxpr/cond
  181.6 23.3 reshape.50
  204.9 6.3 slice.45
  211.3 8.1 copy.68
  244.7 6.3 collective-permute-done.1
  253.0 134.7 %collective-permute-start = (bf16[768,3,128]{2,0,1:T(8,128)(2,1)}, bf16[768,3,128]{2,0,1:T(8,128)(2,1)}, u32[]{:S(2)}, u32[]{:S(2)}) collective-permute-start(bf16[768,3,128]{2,0,1:T(8,128)(2,1)} %copy.138), channel_id=1, source_target_pairs={{0,1},{1,2},{2,3},{3,4},{4,5},{5,6},{6,7},{7,0},{8,9},{9,10},{10,1... | collective-permute-start | bytes 1769480 | tf_op jit(solution)/shard_map/while/body/eval_jaxpr/ppermute | solution.py:69
  397.3 6.3 collective-permute-done.1
  407.5 137.7 %collective-permute-start.1 = (bf16[768,3,128]{2,0,1:T(8,128)(2,1)}, bf16[768,3,128]{2,0,1:T(8,128)(2,1)}, u32[]{:S(2)}, u32[]{:S(2)}) collective-permute-start(bf16[768,3,128]{2,0,1:T(8,128)(2,1)} %copy.139), channel_id=1, source_target_pairs={{0,1},{1,2},{2,3},{3,4},{4,5},{5,6},{6,7},{7,0},{8,9},{9,10},{10,1... | collective-permute-start | bytes 1769480 | tf_op jit(solution)/shard_map/while/body/eval_jaxpr/ppermute | solution.py:70
  551.1 6.3 collective-permute-done.1
  565.8 137.6 %collective-permute-done = bf16[768,3,128]{2,0,1:T(8,128)(2,1)} collective-permute-done((bf16[768,3,128]{2,0,1:T(8,128)(2,1)}, bf16[768,3,128]{2,0,1:T(8,128)(2,1)}, u32[]{:S(2)}, u32[]{:S(2)}) %collective-permute-start) | collective-permute-done | bytes 589856 | tf_op jit(solution)/shard_map/while/body/eval_jaxpr/ppermute | solution.py:69
  703.4 6.3 collective-permute-done.1
  716.7 139.1 %collective-permute-done = bf16[768,3,128]{2,0,1:T(8,128)(2,1)} collective-permute-done((bf16[768,3,128]{2,0,1:T(8,128)(2,1)}, bf16[768,3,128]{2,0,1:T(8,128)(2,1)}, u32[]{:S(2)}, u32[]{:S(2)}) %collective-permute-start) | collective-permute-done | bytes 589856 | tf_op jit(solution)/shard_map/while/body/eval_jaxpr/ppermute | solution.py:69
  855.8 6.3 collective-permute-done.1
  869.1 139.1 %collective-permute-done = bf16[768,3,128]{2,0,1:T(8,128)(2,1)} collective-permute-done((bf16[768,3,128]{2,0,1:T(8,128)(2,1)}, bf16[768,3,128]{2,0,1:T(8,128)(2,1)}, u32[]{:S(2)}, u32[]{:S(2)}) %collective-permute-start) | collective-permute-done | bytes 589856 | tf_op jit(solution)/shard_map/while/body/eval_jaxpr/ppermute | solution.py:69
  1008.2 6.3 collective-permute-done.1
  1018.7 10.4 conditional.4
  1040.9 1927.2 %while.49 = (s32[]{:T(128)}, bf16[768,3,128]{2,0,1:T(8,128)(2,1)}, bf16[768,3,128]{2,0,1:T(8,128)(2,1)}, f32[768,3,128]{2,0,1:T(8,128)}, f32[768,3,128]{2,0,1:T(...) while((s32[]{:T(128)}, bf16[768,3,128]{2,0,1:T(8,128)(2,1)}, ...), condition=%wide.region_14.15_spmd.clone, body=%wide.region_11.14_spmd.clone.sunk | while | flops 5006426112 | bytes 454691008 | solution.py:117
  1048.4 190.1 %conditional.11 = ((f32[768,3,128]{2,0,1:T(8,128)}, f32[768,3,128]{2,0,1:T(8,128)}, f32[768,3,128]{2,0,1:T(8,128)}, f32[768,3,128]{0,2,1:T(8,128)}, f32[8,768,3,128]{3,1,2,0:T(8,128)})) conditional(s32[]{:T(128)} %convert_element_type.129, (f32[768,3,128]{2,0,1:T(8,128)}, f32[768,3,128]{2,0,1:T(8,128)}, f32[768,3,128]{2,0,1:T(8,128)}, ...), branch_computations={%region_12.12_spmd, %region_13.13_spmd} | conditional | flops 5006426112 | bytes 428738272 | solution.py:107
  1050.7 7.0 convolution_bitcast_fusion.1
  1057.7 15.1 copy.36
  1072.8 18.7 copy.74
  1091.5 12.5 slice.46
  1104.1 41.0 %reshape.67 = f32[3536640]{0:T(1024)} reshape(f32[3,1178880]{1,0:T(4,128)} %slice.46) | data formatting | bytes 28293120 | tf_op jit(solution)/shard_map/while/body/eval_jaxpr/cond
  1145.1 23.3 reshape.54
  1185.1 13.8 reshape.69
  1198.9 10.5 reshape.55
  1209.4 8.2 pad.11
  1238.7 283.6 %collective-permute-done.4 = f32[768,3,128]{2,0,1:T(8,128)} collective-permute-done((f32[768,3,128]{2,0,1:T(8,128)}, f32[768,3,128]{2,0,1:T(8,128)}, u32[]{:S(2)}, u32[]{:S(2)}) %collective-permute-start.4) | collective-permute-done | bytes 1179680 | tf_op jit(solution)/shard_map/while/body/eval_jaxpr/ppermute | solution.py:111
  1524.7 10.3 collective-permute-done.5
  1541.2 6.3 collective-permute-done.3
  1556.4 23.0 collective-permute-start.5
  1579.4 135.4 %collective-permute-start.2 = (bf16[768,3,128]{2,0,1:T(8,128)(2,1)}, bf16[768,3,128]{2,0,1:T(8,128)(2,1)}, u32[]{:S(2)}, u32[]{:S(2)}) collective-permute-start(bf16[768,3,128]{2,0,1:T(8,128)(2,1)} %copy.164), channel_id=1, source_target_pairs={{0,1},{1,2},{2,3},{3,4},{4,5},{5,6},{6,7},{7,0},{8,9},{9,10},{10,1... | collective-permute-start | bytes 1769480 | tf_op jit(solution)/shard_map/while/body/eval_jaxpr/ppermute | solution.py:109
  1717.3 40.9 %collective-permute-done.4 = f32[768,3,128]{2,0,1:T(8,128)} collective-permute-done((f32[768,3,128]{2,0,1:T(8,128)}, f32[768,3,128]{2,0,1:T(8,128)}, u32[]{:S(2)}, u32[]{:S(2)}) %collective-permute-start.4) | collective-permute-done | bytes 1179680 | tf_op jit(solution)/shard_map/while/body/eval_jaxpr/ppermute | solution.py:111
  1760.6 10.3 collective-permute-done.5
  1777.2 6.3 collective-permute-done.3
  1790.6 149.9 %collective-permute-start.5 = (f32[768,3,128]{2,0,1:T(8,128)}, f32[768,3,128]{2,0,1:T(8,128)}, u32[]{:S(2)}, u32[]{:S(2)}) collective-permute-start(f32[768,3,128]{2,0,1:T(8,128)} %get-tuple-element.1126), channel_id=1, source_target_pairs={{0,1},{1,2},{2,3},{3,4},{4,5},{5,6},{6,7},{7,0},{8,9},{9,10},{10,1... | collective-permute-start | bytes 3538952 | tf_op jit(solution)/shard_map/while/body/eval_jaxpr/ppermute | solution.py:112
  1940.5 16.5 collective-permute-start.2
  1959.5 35.0 %collective-permute-done.4 = f32[768,3,128]{2,0,1:T(8,128)} collective-permute-done((f32[768,3,128]{2,0,1:T(8,128)}, f32[768,3,128]{2,0,1:T(8,128)}, u32[]{:S(2)}, u32[]{:S(2)}) %collective-permute-start.4) | collective-permute-done | bytes 1179680 | tf_op jit(solution)/shard_map/while/body/eval_jaxpr/ppermute | solution.py:111
  1996.9 10.3 collective-permute-done.5
  2013.5 6.3 collective-permute-done.3
  2026.8 168.6 %collective-permute-start.2 = (bf16[768,3,128]{2,0,1:T(8,128)(2,1)}, bf16[768,3,128]{2,0,1:T(8,128)(2,1)}, u32[]{:S(2)}, u32[]{:S(2)}) collective-permute-start(bf16[768,3,128]{2,0,1:T(8,128)(2,1)} %copy.164), channel_id=1, source_target_pairs={{0,1},{1,2},{2,3},{3,4},{4,5},{5,6},{6,7},{7,0},{8,9},{9,10},{10,1... | collective-permute-start | bytes 1769480 | tf_op jit(solution)/shard_map/while/body/eval_jaxpr/ppermute | solution.py:109
  2197.9 32.3 collective-permute-done.4
  2232.6 10.3 collective-permute-done.5
  2249.2 6.3 collective-permute-done.3
  2262.6 173.9 %collective-permute-start.3 = (bf16[768,3,128]{2,0,1:T(8,128)(2,1)}, bf16[768,3,128]{2,0,1:T(8,128)(2,1)}, u32[]{:S(2)}, u32[]{:S(2)}) collective-permute-start(bf16[768,3,128]{2,0,1:T(8,128)(2,1)} %copy.165), channel_id=1, source_target_pairs={{0,1},{1,2},{2,3},{3,4},{4,5},{5,6},{6,7},{7,0},{8,9},{9,10},{10,1... | collective-permute-start | bytes 1769480 | tf_op jit(solution)/shard_map/while/body/eval_jaxpr/ppermute | solution.py:110
  2436.6 29.7 collective-permute-done.4
  2468.6 10.3 collective-permute-done.5
  2485.2 6.3 collective-permute-done.3
  2498.7 203.8 %collective-permute-done.4 = f32[768,3,128]{2,0,1:T(8,128)} collective-permute-done((f32[768,3,128]{2,0,1:T(8,128)}, f32[768,3,128]{2,0,1:T(8,128)}, u32[]{:S(2)}, u32[]{:S(2)}) %collective-permute-start.4) | collective-permute-done | bytes 1179680 | tf_op jit(solution)/shard_map/while/body/eval_jaxpr/ppermute | solution.py:111
  2704.8 10.3 collective-permute-done.5
  2734.9 203.5 %collective-permute-done.4 = f32[768,3,128]{2,0,1:T(8,128)} collective-permute-done((f32[768,3,128]{2,0,1:T(8,128)}, f32[768,3,128]{2,0,1:T(8,128)}, u32[]{:S(2)}, u32[]{:S(2)}) %collective-permute-start.4) | collective-permute-done | bytes 1179680 | tf_op jit(solution)/shard_map/while/body/eval_jaxpr/ppermute | solution.py:111
  2940.7 10.3 collective-permute-done.5
  2968.1 10.7 conditional.5
  2978.9 274.7 %reduce-scatter.2.cloned.1.call-done = f32[1,768,3,128]{3,1,2,0:T(8,128)} async-done(((f32[8,768,3,128]{3,1,2,0:T(8,128)}), f32[1,768,3,128]{3,1,2,0:T(8,128)}) %reduce-scatter.2.cloned.1.call-update) | async-done | bytes 1179664 | tf_op jit(solution)/shard_map/reduce_scatter | solution.py:122
  3253.7 7.7 rev.7
  3272.4 41.1 %all-reduce.4 = (f32[3,128]{1,0:T(4,128)}, f32[3,128]{1,0:T(4,128)}) all-reduce(f32[3,128]{1,0:T(4,128)S(1)} %get-tuple-element.958, f32[3,128]{1,0:T(4,128)S(1)} %reduce_sum.47), channel_id=1, replica_groups=mesh['hp'=4,'cp'=8] {'cp'}, use_global_device_ids=true, to_apply=%region_18.19 | all-reduce | flops 768 | bytes 6144 | tf_op jit(solution)/shard_map/psum | solution.py:125
  3313.5 24.8 all-reduce.7.cloned.1.call-done
  (248 shorter events, 303.4 us)
Async XLA Ops:
  7.2 4.1 copy-start
  7.2 65.0 %all-gather.3.cloned.1.call-start = ((), (), s32[]{:S(2)}) async-start(), calls=%async_computation.3 | async-start | bytes 5308416 | tf_op jit(solution)/shard_map/all_gather | solution.py:38
  7.2 4.0 copy-start.45
  12.6 9.7 copy-start.43
  12.6 9.7 copy-start.44
  18.4 3235.2 %reduce-scatter.2.cloned.1.call-start = ((), (), s32[]{:S(2)}) async-start(), calls=%async_computation.1 | async-start | bytes 10616832 | tf_op jit(solution)/shard_map/reduce_scatter | solution.py:122
  80.7 151.0 %collective-permute-start = (bf16[768,3,128]{2,0,1:T(8,128)(2,1)}, bf16[768,3,128]{2,0,1:T(8,128)(2,1)}, u32[]{:S(2)}, u32[]{:S(2)}) collective-permute-start(bf16[768,3,128]{2,0,1:T(8,128)(2,1)} %copy.138), channel_id=1, source_target_pairs={{0,1},{1,2},{2,3},{3,4},{4,5},{5,6},{6,7},{7,0},{8,9},{9,10},{10,1... | collective-permute-start | bytes 1769480 | tf_op jit(solution)/shard_map/while/body/eval_jaxpr/ppermute | solution.py:69
  82.9 148.8 %collective-permute-start.1 = (bf16[768,3,128]{2,0,1:T(8,128)(2,1)}, bf16[768,3,128]{2,0,1:T(8,128)(2,1)}, u32[]{:S(2)}, u32[]{:S(2)}) collective-permute-start(bf16[768,3,128]{2,0,1:T(8,128)(2,1)} %copy.139), channel_id=1, source_target_pairs={{0,1},{1,2},{2,3},{3,4},{4,5},{5,6},{6,7},{7,0},{8,9},{9,10},{10,1... | collective-permute-start | bytes 1769480 | tf_op jit(solution)/shard_map/while/body/eval_jaxpr/ppermute | solution.py:70
  222.1 4.9 copy-start.19
  233.6 11.1 collective-permute-start
  235.8 15.3 collective-permute-start.1
  253.0 144.4 %collective-permute-start = (bf16[768,3,128]{2,0,1:T(8,128)(2,1)}, bf16[768,3,128]{2,0,1:T(8,128)(2,1)}, u32[]{:S(2)}, u32[]{:S(2)}) collective-permute-start(bf16[768,3,128]{2,0,1:T(8,128)(2,1)} %copy.138), channel_id=1, source_target_pairs={{0,1},{1,2},{2,3},{3,4},{4,5},{5,6},{6,7},{7,0},{8,9},{9,10},{10,1... | collective-permute-start | bytes 1769480 | tf_op jit(solution)/shard_map/while/body/eval_jaxpr/ppermute | solution.py:69
  389.5 14.1 collective-permute-start.1
  405.6 145.5 %collective-permute-start = (bf16[768,3,128]{2,0,1:T(8,128)(2,1)}, bf16[768,3,128]{2,0,1:T(8,128)(2,1)}, u32[]{:S(2)}, u32[]{:S(2)}) collective-permute-start(bf16[768,3,128]{2,0,1:T(8,128)(2,1)} %copy.138), channel_id=1, source_target_pairs={{0,1},{1,2},{2,3},{3,4},{4,5},{5,6},{6,7},{7,0},{8,9},{9,10},{10,1... | collective-permute-start | bytes 1769480 | tf_op jit(solution)/shard_map/while/body/eval_jaxpr/ppermute | solution.py:69
  407.5 149.9 %collective-permute-start.1 = (bf16[768,3,128]{2,0,1:T(8,128)(2,1)}, bf16[768,3,128]{2,0,1:T(8,128)(2,1)}, u32[]{:S(2)}, u32[]{:S(2)}) collective-permute-start(bf16[768,3,128]{2,0,1:T(8,128)(2,1)} %copy.139), channel_id=1, source_target_pairs={{0,1},{1,2},{2,3},{3,4},{4,5},{5,6},{6,7},{7,0},{8,9},{9,10},{10,1... | collective-permute-start | bytes 1769480 | tf_op jit(solution)/shard_map/while/body/eval_jaxpr/ppermute | solution.py:70
  559.3 144.1 %collective-permute-start = (bf16[768,3,128]{2,0,1:T(8,128)(2,1)}, bf16[768,3,128]{2,0,1:T(8,128)(2,1)}, u32[]{:S(2)}, u32[]{:S(2)}) collective-permute-start(bf16[768,3,128]{2,0,1:T(8,128)(2,1)} %copy.138), channel_id=1, source_target_pairs={{0,1},{1,2},{2,3},{3,4},{4,5},{5,6},{6,7},{7,0},{8,9},{9,10},{10,1... | collective-permute-start | bytes 1769480 | tf_op jit(solution)/shard_map/while/body/eval_jaxpr/ppermute | solution.py:69
  561.2 148.5 %collective-permute-start.1 = (bf16[768,3,128]{2,0,1:T(8,128)(2,1)}, bf16[768,3,128]{2,0,1:T(8,128)(2,1)}, u32[]{:S(2)}, u32[]{:S(2)}) collective-permute-start(bf16[768,3,128]{2,0,1:T(8,128)(2,1)} %copy.139), channel_id=1, source_target_pairs={{0,1},{1,2},{2,3},{3,4},{4,5},{5,6},{6,7},{7,0},{8,9},{9,10},{10,1... | collective-permute-start | bytes 1769480 | tf_op jit(solution)/shard_map/while/body/eval_jaxpr/ppermute | solution.py:70
  711.7 144.1 %collective-permute-start = (bf16[768,3,128]{2,0,1:T(8,128)(2,1)}, bf16[768,3,128]{2,0,1:T(8,128)(2,1)}, u32[]{:S(2)}, u32[]{:S(2)}) collective-permute-start(bf16[768,3,128]{2,0,1:T(8,128)(2,1)} %copy.138), channel_id=1, source_target_pairs={{0,1},{1,2},{2,3},{3,4},{4,5},{5,6},{6,7},{7,0},{8,9},{9,10},{10,1... | collective-permute-start | bytes 1769480 | tf_op jit(solution)/shard_map/while/body/eval_jaxpr/ppermute | solution.py:69
  713.6 148.5 %collective-permute-start.1 = (bf16[768,3,128]{2,0,1:T(8,128)(2,1)}, bf16[768,3,128]{2,0,1:T(8,128)(2,1)}, u32[]{:S(2)}, u32[]{:S(2)}) collective-permute-start(bf16[768,3,128]{2,0,1:T(8,128)(2,1)} %copy.139), channel_id=1, source_target_pairs={{0,1},{1,2},{2,3},{3,4},{4,5},{5,6},{6,7},{7,0},{8,9},{9,10},{10,1... | collective-permute-start | bytes 1769480 | tf_op jit(solution)/shard_map/while/body/eval_jaxpr/ppermute | solution.py:70
  864.0 144.1 %collective-permute-start = (bf16[768,3,128]{2,0,1:T(8,128)(2,1)}, bf16[768,3,128]{2,0,1:T(8,128)(2,1)}, u32[]{:S(2)}, u32[]{:S(2)}) collective-permute-start(bf16[768,3,128]{2,0,1:T(8,128)(2,1)} %copy.138), channel_id=1, source_target_pairs={{0,1},{1,2},{2,3},{3,4},{4,5},{5,6},{6,7},{7,0},{8,9},{9,10},{10,1... | collective-permute-start | bytes 1769480 | tf_op jit(solution)/shard_map/while/body/eval_jaxpr/ppermute | solution.py:69
  866.0 148.5 %collective-permute-start.1 = (bf16[768,3,128]{2,0,1:T(8,128)(2,1)}, bf16[768,3,128]{2,0,1:T(8,128)(2,1)}, u32[]{:S(2)}, u32[]{:S(2)}) collective-permute-start(bf16[768,3,128]{2,0,1:T(8,128)(2,1)} %copy.139), channel_id=1, source_target_pairs={{0,1},{1,2},{2,3},{3,4},{4,5},{5,6},{6,7},{7,0},{8,9},{9,10},{10,1... | collective-permute-start | bytes 1769480 | tf_op jit(solution)/shard_map/while/body/eval_jaxpr/ppermute | solution.py:70
  1168.4 2.8 copy-start.4
  1171.2 7.3 copy-start.6
  1171.2 7.3 copy-start.26
  1175.6 2.9 copy-start.3
  1226.8 2.8 copy-start.2
  1226.8 2.8 copy-start.15
  1229.6 5.8 copy-start.32
  1229.6 5.8 slice-start
  1231.4 4.0 copy-start.16
  1231.4 4.0 slice-start.1
  1231.4 4.0 copy-start.7
  1231.4 4.0 copy-start.10
  1238.4 283.9 %collective-permute-start.4 = (f32[768,3,128]{2,0,1:T(8,128)}, f32[768,3,128]{2,0,1:T(8,128)}, u32[]{:S(2)}, u32[]{:S(2)}) collective-permute-start(f32[768,3,128]{2,0,1:T(8,128)} %get-tuple-element.1125), channel_id=1, source_target_pairs={{0,1},{1,2},{2,3},{3,4},{4,5},{5,6},{6,7},{7,0},{8,9},{9,10},{10,1... | collective-permute-start | bytes 3538952 | tf_op jit(solution)/shard_map/while/body/eval_jaxpr/ppermute | solution.py:111
  1238.5 296.4 %collective-permute-start.5 = (f32[768,3,128]{2,0,1:T(8,128)}, f32[768,3,128]{2,0,1:T(8,128)}, u32[]{:S(2)}, u32[]{:S(2)}) collective-permute-start(f32[768,3,128]{2,0,1:T(8,128)} %get-tuple-element.1126), channel_id=1, source_target_pairs={{0,1},{1,2},{2,3},{3,4},{4,5},{5,6},{6,7},{7,0},{8,9},{9,10},{10,1... | collective-permute-start | bytes 3538952 | tf_op jit(solution)/shard_map/while/body/eval_jaxpr/ppermute | solution.py:112
  1238.6 302.7 %collective-permute-start.2 = (bf16[768,3,128]{2,0,1:T(8,128)(2,1)}, bf16[768,3,128]{2,0,1:T(8,128)(2,1)}, u32[]{:S(2)}, u32[]{:S(2)}) collective-permute-start(bf16[768,3,128]{2,0,1:T(8,128)(2,1)} %copy.164), channel_id=1, source_target_pairs={{0,1},{1,2},{2,3},{3,4},{4,5},{5,6},{6,7},{7,0},{8,9},{9,10},{10,1... | collective-permute-start | bytes 1769480 | tf_op jit(solution)/shard_map/while/body/eval_jaxpr/ppermute | solution.py:109
  1238.6 308.9 %collective-permute-start.3 = (bf16[768,3,128]{2,0,1:T(8,128)(2,1)}, bf16[768,3,128]{2,0,1:T(8,128)(2,1)}, u32[]{:S(2)}, u32[]{:S(2)}) collective-permute-start(bf16[768,3,128]{2,0,1:T(8,128)(2,1)} %copy.165), channel_id=1, source_target_pairs={{0,1},{1,2},{2,3},{3,4},{4,5},{5,6},{6,7},{7,0},{8,9},{9,10},{10,1... | collective-permute-start | bytes 1769480 | tf_op jit(solution)/shard_map/while/body/eval_jaxpr/ppermute | solution.py:110
  1556.3 201.9 %collective-permute-start.4 = (f32[768,3,128]{2,0,1:T(8,128)}, f32[768,3,128]{2,0,1:T(8,128)}, u32[]{:S(2)}, u32[]{:S(2)}) collective-permute-start(f32[768,3,128]{2,0,1:T(8,128)} %get-tuple-element.1125), channel_id=1, source_target_pairs={{0,1},{1,2},{2,3},{3,4},{4,5},{5,6},{6,7},{7,0},{8,9},{9,10},{10,1... | collective-permute-start | bytes 3538952 | tf_op jit(solution)/shard_map/while/body/eval_jaxpr/ppermute | solution.py:111
  1556.4 214.5 %collective-permute-start.5 = (f32[768,3,128]{2,0,1:T(8,128)}, f32[768,3,128]{2,0,1:T(8,128)}, u32[]{:S(2)}, u32[]{:S(2)}) collective-permute-start(f32[768,3,128]{2,0,1:T(8,128)} %get-tuple-element.1126), channel_id=1, source_target_pairs={{0,1},{1,2},{2,3},{3,4},{4,5},{5,6},{6,7},{7,0},{8,9},{9,10},{10,1... | collective-permute-start | bytes 3538952 | tf_op jit(solution)/shard_map/while/body/eval_jaxpr/ppermute | solution.py:112
  1579.4 197.8 %collective-permute-start.2 = (bf16[768,3,128]{2,0,1:T(8,128)(2,1)}, bf16[768,3,128]{2,0,1:T(8,128)(2,1)}, u32[]{:S(2)}, u32[]{:S(2)}) collective-permute-start(bf16[768,3,128]{2,0,1:T(8,128)(2,1)} %copy.164), channel_id=1, source_target_pairs={{0,1},{1,2},{2,3},{3,4},{4,5},{5,6},{6,7},{7,0},{8,9},{9,10},{10,1... | collective-permute-start | bytes 1769480 | tf_op jit(solution)/shard_map/while/body/eval_jaxpr/ppermute | solution.py:109
  1714.8 68.7 %collective-permute-start.3 = (bf16[768,3,128]{2,0,1:T(8,128)(2,1)}, bf16[768,3,128]{2,0,1:T(8,128)(2,1)}, u32[]{:S(2)}, u32[]{:S(2)}) collective-permute-start(bf16[768,3,128]{2,0,1:T(8,128)(2,1)} %copy.165), channel_id=1, source_target_pairs={{0,1},{1,2},{2,3},{3,4},{4,5},{5,6},{6,7},{7,0},{8,9},{9,10},{10,1... | collective-permute-start | bytes 1769480 | tf_op jit(solution)/shard_map/while/body/eval_jaxpr/ppermute | solution.py:110
  1790.6 203.9 %collective-permute-start.4 = (f32[768,3,128]{2,0,1:T(8,128)}, f32[768,3,128]{2,0,1:T(8,128)}, u32[]{:S(2)}, u32[]{:S(2)}) collective-permute-start(f32[768,3,128]{2,0,1:T(8,128)} %get-tuple-element.1125), channel_id=1, source_target_pairs={{0,1},{1,2},{2,3},{3,4},{4,5},{5,6},{6,7},{7,0},{8,9},{9,10},{10,1... | collective-permute-start | bytes 3538952 | tf_op jit(solution)/shard_map/while/body/eval_jaxpr/ppermute | solution.py:111
  1790.6 216.6 %collective-permute-start.5 = (f32[768,3,128]{2,0,1:T(8,128)}, f32[768,3,128]{2,0,1:T(8,128)}, u32[]{:S(2)}, u32[]{:S(2)}) collective-permute-start(f32[768,3,128]{2,0,1:T(8,128)} %get-tuple-element.1126), channel_id=1, source_target_pairs={{0,1},{1,2},{2,3},{3,4},{4,5},{5,6},{6,7},{7,0},{8,9},{9,10},{10,1... | collective-permute-start | bytes 3538952 | tf_op jit(solution)/shard_map/while/body/eval_jaxpr/ppermute | solution.py:112
  1940.5 72.9 %collective-permute-start.2 = (bf16[768,3,128]{2,0,1:T(8,128)(2,1)}, bf16[768,3,128]{2,0,1:T(8,128)(2,1)}, u32[]{:S(2)}, u32[]{:S(2)}) collective-permute-start(bf16[768,3,128]{2,0,1:T(8,128)(2,1)} %copy.164), channel_id=1, source_target_pairs={{0,1},{1,2},{2,3},{3,4},{4,5},{5,6},{6,7},{7,0},{8,9},{9,10},{10,1... | collective-permute-start | bytes 1769480 | tf_op jit(solution)/shard_map/while/body/eval_jaxpr/ppermute | solution.py:109
  1957.0 62.8 %collective-permute-start.3 = (bf16[768,3,128]{2,0,1:T(8,128)(2,1)}, bf16[768,3,128]{2,0,1:T(8,128)(2,1)}, u32[]{:S(2)}, u32[]{:S(2)}) collective-permute-start(bf16[768,3,128]{2,0,1:T(8,128)(2,1)} %copy.165), channel_id=1, source_target_pairs={{0,1},{1,2},{2,3},{3,4},{4,5},{5,6},{6,7},{7,0},{8,9},{9,10},{10,1... | collective-permute-start | bytes 1769480 | tf_op jit(solution)/shard_map/while/body/eval_jaxpr/ppermute | solution.py:110
  2026.8 203.5 %collective-permute-start.4 = (f32[768,3,128]{2,0,1:T(8,128)}, f32[768,3,128]{2,0,1:T(8,128)}, u32[]{:S(2)}, u32[]{:S(2)}) collective-permute-start(f32[768,3,128]{2,0,1:T(8,128)} %get-tuple-element.1125), channel_id=1, source_target_pairs={{0,1},{1,2},{2,3},{3,4},{4,5},{5,6},{6,7},{7,0},{8,9},{9,10},{10,1... | collective-permute-start | bytes 3538952 | tf_op jit(solution)/shard_map/while/body/eval_jaxpr/ppermute | solution.py:111
  2026.8 216.1 %collective-permute-start.5 = (f32[768,3,128]{2,0,1:T(8,128)}, f32[768,3,128]{2,0,1:T(8,128)}, u32[]{:S(2)}, u32[]{:S(2)}) collective-permute-start(f32[768,3,128]{2,0,1:T(8,128)} %get-tuple-element.1126), channel_id=1, source_target_pairs={{0,1},{1,2},{2,3},{3,4},{4,5},{5,6},{6,7},{7,0},{8,9},{9,10},{10,1... | collective-permute-start | bytes 3538952 | tf_op jit(solution)/shard_map/while/body/eval_jaxpr/ppermute | solution.py:112
  2026.8 222.4 %collective-permute-start.2 = (bf16[768,3,128]{2,0,1:T(8,128)(2,1)}, bf16[768,3,128]{2,0,1:T(8,128)(2,1)}, u32[]{:S(2)}, u32[]{:S(2)}) collective-permute-start(bf16[768,3,128]{2,0,1:T(8,128)(2,1)} %copy.164), channel_id=1, source_target_pairs={{0,1},{1,2},{2,3},{3,4},{4,5},{5,6},{6,7},{7,0},{8,9},{9,10},{10,1... | collective-permute-start | bytes 1769480 | tf_op jit(solution)/shard_map/while/body/eval_jaxpr/ppermute | solution.py:109
  2195.4 60.1 %collective-permute-start.3 = (bf16[768,3,128]{2,0,1:T(8,128)(2,1)}, bf16[768,3,128]{2,0,1:T(8,128)(2,1)}, u32[]{:S(2)}, u32[]{:S(2)}) collective-permute-start(bf16[768,3,128]{2,0,1:T(8,128)(2,1)} %copy.165), channel_id=1, source_target_pairs={{0,1},{1,2},{2,3},{3,4},{4,5},{5,6},{6,7},{7,0},{8,9},{9,10},{10,1... | collective-permute-start | bytes 1769480 | tf_op jit(solution)/shard_map/while/body/eval_jaxpr/ppermute | solution.py:110
  2262.6 203.7 %collective-permute-start.4 = (f32[768,3,128]{2,0,1:T(8,128)}, f32[768,3,128]{2,0,1:T(8,128)}, u32[]{:S(2)}, u32[]{:S(2)}) collective-permute-start(f32[768,3,128]{2,0,1:T(8,128)} %get-tuple-element.1125), channel_id=1, source_target_pairs={{0,1},{1,2},{2,3},{3,4},{4,5},{5,6},{6,7},{7,0},{8,9},{9,10},{10,1... | collective-permute-start | bytes 3538952 | tf_op jit(solution)/shard_map/while/body/eval_jaxpr/ppermute | solution.py:111
  2262.6 216.3 %collective-permute-start.5 = (f32[768,3,128]{2,0,1:T(8,128)}, f32[768,3,128]{2,0,1:T(8,128)}, u32[]{:S(2)}, u32[]{:S(2)}) collective-permute-start(f32[768,3,128]{2,0,1:T(8,128)} %get-tuple-element.1126), channel_id=1, source_target_pairs={{0,1},{1,2},{2,3},{3,4},{4,5},{5,6},{6,7},{7,0},{8,9},{9,10},{10,1... | collective-permute-start | bytes 3538952 | tf_op jit(solution)/shard_map/while/body/eval_jaxpr/ppermute | solution.py:112
  2262.6 222.6 %collective-permute-start.2 = (bf16[768,3,128]{2,0,1:T(8,128)(2,1)}, bf16[768,3,128]{2,0,1:T(8,128)(2,1)}, u32[]{:S(2)}, u32[]{:S(2)}) collective-permute-start(bf16[768,3,128]{2,0,1:T(8,128)(2,1)} %copy.164), channel_id=1, source_target_pairs={{0,1},{1,2},{2,3},{3,4},{4,5},{5,6},{6,7},{7,0},{8,9},{9,10},{10,1... | collective-permute-start | bytes 1769480 | tf_op jit(solution)/shard_map/while/body/eval_jaxpr/ppermute | solution.py:109
  2262.6 228.9 %collective-permute-start.3 = (bf16[768,3,128]{2,0,1:T(8,128)(2,1)}, bf16[768,3,128]{2,0,1:T(8,128)(2,1)}, u32[]{:S(2)}, u32[]{:S(2)}) collective-permute-start(bf16[768,3,128]{2,0,1:T(8,128)(2,1)} %copy.165), channel_id=1, source_target_pairs={{0,1},{1,2},{2,3},{3,4},{4,5},{5,6},{6,7},{7,0},{8,9},{9,10},{10,1... | collective-permute-start | bytes 1769480 | tf_op jit(solution)/shard_map/while/body/eval_jaxpr/ppermute | solution.py:110
  2498.5 203.9 %collective-permute-start.4 = (f32[768,3,128]{2,0,1:T(8,128)}, f32[768,3,128]{2,0,1:T(8,128)}, u32[]{:S(2)}, u32[]{:S(2)}) collective-permute-start(f32[768,3,128]{2,0,1:T(8,128)} %get-tuple-element.1125), channel_id=1, source_target_pairs={{0,1},{1,2},{2,3},{3,4},{4,5},{5,6},{6,7},{7,0},{8,9},{9,10},{10,1... | collective-permute-start | bytes 3538952 | tf_op jit(solution)/shard_map/while/body/eval_jaxpr/ppermute | solution.py:111
  2498.5 216.5 %collective-permute-start.5 = (f32[768,3,128]{2,0,1:T(8,128)}, f32[768,3,128]{2,0,1:T(8,128)}, u32[]{:S(2)}, u32[]{:S(2)}) collective-permute-start(f32[768,3,128]{2,0,1:T(8,128)} %get-tuple-element.1126), channel_id=1, source_target_pairs={{0,1},{1,2},{2,3},{3,4},{4,5},{5,6},{6,7},{7,0},{8,9},{9,10},{10,1... | collective-permute-start | bytes 3538952 | tf_op jit(solution)/shard_map/while/body/eval_jaxpr/ppermute | solution.py:112
  2498.5 222.9 %collective-permute-start.2 = (bf16[768,3,128]{2,0,1:T(8,128)(2,1)}, bf16[768,3,128]{2,0,1:T(8,128)(2,1)}, u32[]{:S(2)}, u32[]{:S(2)}) collective-permute-start(bf16[768,3,128]{2,0,1:T(8,128)(2,1)} %copy.164), channel_id=1, source_target_pairs={{0,1},{1,2},{2,3},{3,4},{4,5},{5,6},{6,7},{7,0},{8,9},{9,10},{10,1... | collective-permute-start | bytes 1769480 | tf_op jit(solution)/shard_map/while/body/eval_jaxpr/ppermute | solution.py:109
  2498.6 229.1 %collective-permute-start.3 = (bf16[768,3,128]{2,0,1:T(8,128)(2,1)}, bf16[768,3,128]{2,0,1:T(8,128)(2,1)}, u32[]{:S(2)}, u32[]{:S(2)}) collective-permute-start(bf16[768,3,128]{2,0,1:T(8,128)(2,1)} %copy.165), channel_id=1, source_target_pairs={{0,1},{1,2},{2,3},{3,4},{4,5},{5,6},{6,7},{7,0},{8,9},{9,10},{10,1... | collective-permute-start | bytes 1769480 | tf_op jit(solution)/shard_map/while/body/eval_jaxpr/ppermute | solution.py:110
  2734.7 203.6 %collective-permute-start.4 = (f32[768,3,128]{2,0,1:T(8,128)}, f32[768,3,128]{2,0,1:T(8,128)}, u32[]{:S(2)}, u32[]{:S(2)}) collective-permute-start(f32[768,3,128]{2,0,1:T(8,128)} %get-tuple-element.1125), channel_id=1, source_target_pairs={{0,1},{1,2},{2,3},{3,4},{4,5},{5,6},{6,7},{7,0},{8,9},{9,10},{10,1... | collective-permute-start | bytes 3538952 | tf_op jit(solution)/shard_map/while/body/eval_jaxpr/ppermute | solution.py:111
  2734.7 216.2 %collective-permute-start.5 = (f32[768,3,128]{2,0,1:T(8,128)}, f32[768,3,128]{2,0,1:T(8,128)}, u32[]{:S(2)}, u32[]{:S(2)}) collective-permute-start(f32[768,3,128]{2,0,1:T(8,128)} %get-tuple-element.1126), channel_id=1, source_target_pairs={{0,1},{1,2},{2,3},{3,4},{4,5},{5,6},{6,7},{7,0},{8,9},{9,10},{10,1... | collective-permute-start | bytes 3538952 | tf_op jit(solution)/shard_map/while/body/eval_jaxpr/ppermute | solution.py:112
  2734.7 222.6 %collective-permute-start.2 = (bf16[768,3,128]{2,0,1:T(8,128)(2,1)}, bf16[768,3,128]{2,0,1:T(8,128)(2,1)}, u32[]{:S(2)}, u32[]{:S(2)}) collective-permute-start(bf16[768,3,128]{2,0,1:T(8,128)(2,1)} %copy.164), channel_id=1, source_target_pairs={{0,1},{1,2},{2,3},{3,4},{4,5},{5,6},{6,7},{7,0},{8,9},{9,10},{10,1... | collective-permute-start | bytes 1769480 | tf_op jit(solution)/shard_map/while/body/eval_jaxpr/ppermute | solution.py:109
  2734.8 228.8 %collective-permute-start.3 = (bf16[768,3,128]{2,0,1:T(8,128)(2,1)}, bf16[768,3,128]{2,0,1:T(8,128)(2,1)}, u32[]{:S(2)}, u32[]{:S(2)}) collective-permute-start(bf16[768,3,128]{2,0,1:T(8,128)(2,1)} %copy.165), channel_id=1, source_target_pairs={{0,1},{1,2},{2,3},{3,4},{4,5},{5,6},{6,7},{7,0},{8,9},{9,10},{10,1... | collective-permute-start | bytes 1769480 | tf_op jit(solution)/shard_map/while/body/eval_jaxpr/ppermute | solution.py:110
  2978.9 359.4 %all-reduce.7.cloned.1.call-start = ((), (), s32[]{:S(2)}) async-start(), calls=%async_computation.2 | async-start | bytes 4718592 | tf_op jit(solution)/shard_map/psum | solution.py:124
  3266.2 47.3 %collective-permute-start.6 = (bf16[768,3,128]{2,0,1:T(8,128)(2,1)}, bf16[768,3,128]{2,0,1:T(8,128)(2,1)}, u32[]{:S(2)}, u32[]{:S(2)}) collective-permute-start(bf16[768,3,128]{2,0,1:T(8,128)(2,1)} %convert.10), channel_id=1, source_target_pairs={{0,1},{1,2},{2,3},{3,4},{4,5},{5,6},{6,7},{7,0},{8,9},{9,10},{10,1... | collective-permute-start | bytes 1769480 | tf_op jit(solution)/shard_map/ppermute | solution.py:120
  3267.1 46.4 %collective-permute-start.7 = (bf16[768,3,128]{2,0,1:T(8,128)(2,1)}, bf16[768,3,128]{2,0,1:T(8,128)(2,1)}, u32[]{:S(2)}, u32[]{:S(2)}) collective-permute-start(bf16[768,3,128]{2,0,1:T(8,128)(2,1)} %convert.11), channel_id=1, source_target_pairs={{0,1},{1,2},{2,3},{3,4},{4,5},{5,6},{6,7},{7,0},{8,9},{9,10},{10,1... | collective-permute-start | bytes 1769480 | tf_op jit(solution)/shard_map/ppermute | solution.py:121
  (12 other events, 16.4 us)
Sparse Core Ops, SparseCore 0:
  18.5 53.6 all-gather.2
  2979.0 274.6 reduce-scatter.1
  3264.0 74.2 all-reduce.6
where the time goes:
time: 3390 us; the launch traced here: 3350 us
  waiting for transfers between devices  1790 us (53%)
  starting transfers between devices  952 us (28%)
  local copies, waits for them, and re-layouts  462 us (14%)
  matrix products  45 us (1%)
  blocking collectives  41.1 us (1%)
    ppermute x7, waiting for transfers between devices, bwd_step(): dk_acc = lax.ppermute(dk_acc, 'cp', shift_pairs)  829 us
    ppermute x7, waiting for transfers between devices, fwd_step(): k_blk = lax.ppermute(k_blk, 'cp', shift_pairs)  427 us
    ppermute x7, starting transfers between devices, bwd_step(): k_blk = lax.ppermute(k_blk, 'cp', shift_pairs)  321 us
    reduce_scatter x1, waiting for transfers between devices, local_fn(): lax.psum_scatter(grad_rel, 'cp', scatter_dimension=0, tiled=False)  275 us
    ppermute x7, starting transfers between devices, bwd_step(): v_blk = lax.ppermute(v_blk, 'cp', shift_pairs)  182 us
    ppermute x7, starting transfers between devices, bwd_step(): dv_acc = lax.ppermute(dv_acc, 'cp', shift_pairs)  173 us
    cond x55, local copies, waits for them, and re-layouts  149 us
    ppermute x7, starting transfers between devices, fwd_step(): v_blk = lax.ppermute(v_blk, 'cp', shift_pairs)  141 us
  transfers between devices with their start and end apart: 47, of which 43 were waited for; matrix products, arithmetic and copies ran while one was open for 7% of the time, Pallas kernels for 0%

commit v1 on v0

v1 whole, which is shorter than its diff:
```python
import functools
import math

import jax
import jax.numpy as jnp
from jax import lax
from jax.experimental import pallas as pl
from jax.experimental.pallas import tpu as pltpu
from jax.sharding import PartitionSpec as P

F32, BF16 = jnp.float32, jnp.bfloat16
ROWS = 256
COLS = 512
NT = (((1,), (1,)), ((), ()))
NN = (((1,), (0,)), ((), ()))


def mm(a, b, dims=NN, precision=None):
    return lax.dot_general(a, b, dims, preferred_element_type=F32, precision=precision)


def fold_lanes(op, x):
    acc = x[:, :128]
    for g in range(1, x.shape[1] // 128):
        acc = op(acc, x[:, g * 128:(g + 1) * 128])
    return acc


def shear(window, shift):
    half = window.shape[0] // 2
    width = window.shape[1]
    top = pltpu.roll(window[:half, 128:], shift, 1, stride=1, stride_axis=0)[:, 128:]
    low = pltpu.roll(window[half:, :width - 128], shift, 1, stride=1, stride_axis=0)[:, 128:]
    return jnp.concatenate([top, low], axis=0)


def tile_grads(q0, out_row, q_ref, k_ref, v_ref, do_ref, rel_ref, bias_ref, o_ref, dq_ref, dkt, dvt, drt, bias_acc, buf, m_ref, l_ref, acc_ref, gu_ref, gv_ref):
    seq, dim = k_ref.shape
    scale = dim ** -0.5
    steps = (q0 + ROWS + COLS - 1) // COLS
    rel0 = seq - ROWS - q0

    def at(base, size):
        return pl.ds(pl.multiple_of(base, ROWS), size)

    q_wide = q_ref[at(q0, ROWS), :].astype(F32)
    q_u = (q_wide + bias_ref[0:1, :]).astype(BF16)
    q_v = (q_wide + bias_ref[1:2, :]).astype(BF16)

    @pl.loop(0, steps)
    def _(c):
        buf[:, at(c * COLS + ROWS, COLS)] = mm(q_v, rel_ref[at(rel0 + c * COLS, COLS), :], NT)

    m_ref[...] = jnp.full_like(m_ref, -jnp.inf)
    row_minus_col = lax.broadcasted_iota(jnp.int32, (ROWS, COLS), 0) - lax.broadcasted_iota(jnp.int32, (ROWS, COLS), 1)

    @pl.loop(0, steps)
    def _(c):
        j0 = c * COLS
        score = mm(q_u, k_ref[at(j0, COLS), :], NT) + shear(buf[:, at(j0 + ROWS, COLS + ROWS)], 1)
        score = jnp.where(row_minus_col >= j0 - q0, score, -jnp.inf)
        buf[:, at(j0 + ROWS, COLS)] = score
        m_ref[...] = jnp.maximum(m_ref[...], fold_lanes(jnp.maximum, score))

    row_max = jnp.max(m_ref[...], axis=1, keepdims=True)
    l_ref[...] = jnp.zeros_like(l_ref)
    acc_ref[...] = jnp.zeros_like(acc_ref)

    @pl.loop(0, steps)
    def _(c):
        j0 = c * COLS
        prob = jnp.exp2((buf[:, at(j0 + ROWS, COLS)] - row_max) * (scale * math.log2(math.e)))
        buf[:, at(j0 + ROWS, COLS)] = prob
        l_ref[...] += fold_lanes(jnp.add, prob)
        acc_ref[...] += mm(prob.astype(BF16), v_ref[at(j0, COLS), :])

    inv_sum = 1.0 / jnp.sum(l_ref[...], axis=1, keepdims=True)
    out = acc_ref[...] * inv_sum
    o_ref[at(out_row, ROWS), :] = out.astype(BF16)
    d_out = do_ref[at(q0, ROWS), :]
    do_wide = d_out.astype(F32)
    delta = jnp.sum(do_wide * out, axis=1, keepdims=True)
    anti = (lax.broadcasted_iota(jnp.int32, (ROWS, ROWS), 0) + lax.broadcasted_iota(jnp.int32, (ROWS, ROWS), 1) == ROWS - 1)
    anti_b = anti.astype(F32).astype(BF16)
    do_t = do_wide.T.astype(BF16)
    qu_t = q_u.astype(F32).T.astype(BF16)
    qv_rt = mm(anti_b, q_v).T.astype(BF16)
    gu_ref[...] = jnp.zeros_like(gu_ref)
    gv_ref[...] = jnp.zeros_like(gv_ref)

    @pl.loop(0, steps)
    def _(c):
        j0 = c * COLS
        cols = at(j0, COLS)
        prob = buf[:, at(j0 + ROWS, COLS)] * inv_sum
        ds = (prob * (mm(d_out, v_ref[cols, :], NT) - delta)).astype(BF16)
        buf[:, at(j0 + ROWS, COLS)] = mm(anti_b, ds)
        dvt[:, cols] += mm(do_t, prob.astype(BF16))
        dkt[:, cols] += mm(qu_t, ds)
        gu_ref[...] += mm(ds, k_ref[cols, :])

    @pl.loop(0, steps)
    def _(c):
        c0 = c * COLS
        by_offset = shear(buf[:, at(c0, COLS + ROWS)], 0).astype(BF16)
        cols = at(rel0 + c0, COLS)
        gv_ref[...] += mm(by_offset, rel_ref[cols, :])
        drt[:, cols] += mm(qv_rt, by_offset)

    g_u = gu_ref[...]
    g_vr = gv_ref[...]
    g_v = mm(anti.astype(F32), g_vr, precision=lax.Precision.HIGHEST)
    dq_ref[at(out_row, ROWS), :] = ((g_u + g_v) * scale).astype(BF16)
    bias_acc[0:1, :] += jnp.sum(g_u, axis=0, keepdims=True) * scale
    bias_acc[1:2, :] += jnp.sum(g_vr, axis=0, keepdims=True) * scale


def tile_index(i, core):
    return 4 * (i // 2) + jnp.where(i % 2 == 0, core, 3 - core)


def group_kernel(xs, rels, bias_ref, o_out, g_out, bias_acc, xh, relh, dkt, dvt, drt, part, red, o_tiles, *rest):
    scratch, sems = rest[:6], rest[6:]
    in_send, in_recv, fwd_send, fwd_recv, part_send, part_recv, tile_send, red_send, out_recv, g_recv = sems
    n_arr, n_heads, block, dim = xs.shape
    n_dev = lax.axis_size('cp')
    n_chips = n_dev // 2
    seq = block * n_dev
    scale = dim ** -0.5
    me = lax.axis_index('cp')
    chip, core = me // 2, me % 2
    head = jnp.minimum(chip, n_heads - 1)
    active = chip < n_heads
    partner = 2 * chip + 1 - core
    n_tiles = seq // ROWS // 2

    barrier = pltpu.get_barrier_semaphore()
    for d in range(1, n_dev):
        pl.semaphore_signal(barrier, inc=1, device_id={'cp': (me + d) % n_dev}, device_id_type=pl.DeviceIdType.MESH)
    pl.semaphore_wait(barrier, n_dev - 1)

    def push(src, dst, send, recv, dev):
        return pltpu.make_async_remote_copy(src_ref=src, dst_ref=dst, send_sem=send, recv_sem=recv, device_id={'cp': dev}, device_id_type=pl.DeviceIdType.MESH)

    def rows_of(dev):
        return pl.ds(pl.multiple_of(dev * block, block), block)

    def flip_rows_of(dev):
        return pl.ds(pl.multiple_of(seq - block - dev * block, block), block)

    def input_pair(dest_head, src_dev, x_src, rel_src, send, recv, dev):
        return (
            push(x_src, xh.at[:, rows_of(src_dev), :], send.at[0], recv.at[0], dev),
            push(rel_src, relh.at[flip_rows_of(src_dev), :], send.at[1], recv.at[1], dev),
        )

    def send_to(dest_head):
        return input_pair(dest_head, me, xs.at[:, dest_head], rels.at[dest_head], in_send.at[dest_head], in_recv.at[chip], 2 * dest_head + core)

    def relay(src_chip):
        src_dev = 2 * src_chip + core
        return input_pair(head, src_dev, xh.at[:, rows_of(src_dev), :], relh.at[flip_rows_of(src_dev), :], fwd_send.at[src_chip], fwd_recv.at[src_chip], partner)

    def relay_own():
        return input_pair(head, me, xs.at[:, head], rels.at[head], fwd_send.at[chip], fwd_recv.at[chip], partner)

    def local_own():
        return (
            pltpu.make_async_copy(xs.at[:, head], xh.at[:, rows_of(me), :], in_recv.at[chip, 0]),
            pltpu.make_async_copy(rels.at[head], relh.at[flip_rows_of(me), :], in_recv.at[chip, 1]),
        )

    for dest in range(n_heads):
        @pl.when(chip != dest)
        def _():
            for copy in send_to(dest):
                copy.start()

    dkt[...] = jnp.zeros_like(dkt)
    dvt[...] = jnp.zeros_like(dvt)
    drt[...] = jnp.zeros_like(drt)
    bias_acc[...] = jnp.zeros_like(bias_acc)
    scratch[0][:, :ROWS] = jnp.zeros((ROWS, ROWS), F32)
    relh[pl.ds(seq, COLS), :] = jnp.zeros((COLS, dim), BF16)

    @pl.when(active)
    def _():
        for copy in local_own():
            copy.start()
        for copy in relay_own():
            copy.start()
        for src in range(n_chips):
            @pl.when(chip != src)
            def _():
                x_in, rel_in = input_pair(head, 2 * src + core, xs.at[:, head], rels.at[head], in_send.at[0], in_recv.at[src], partner)
                x_in.wait_recv()
                rel_in.wait_recv()
                for copy in relay(src):
                    copy.start()
        for copy in local_own():
            copy.wait()
        for src in range(n_chips):
            x_in, rel_in = input_pair(head, 2 * src + 1 - core, xs.at[:, head], rels.at[head], fwd_send.at[src], fwd_recv.at[src], partner)
            x_in.wait_recv()
            rel_in.wait_recv()

    q_ref, k_ref, v_ref, do_ref = (xh.at[a] for a in range(4))

    @pl.when(active)
    def _():
        @pl.loop(0, n_tiles)
        def _(i):
            tile_grads(tile_index(i, core) * ROWS, i * ROWS, q_ref, k_ref, v_ref, do_ref, relh, bias_ref.at[head], o_tiles.at[0], o_tiles.at[1], dkt, dvt, drt, bias_acc, *scratch)

        def part_copy(a, src_chip, parity):
            dev = 2 * src_chip + parity
            acc = (dkt, dvt, drt)[a]
            cols = flip_rows_of(dev) if a == 2 else rows_of(dev)
            return push(acc.at[:, cols], part.at[a, src_chip], part_send.at[a, src_chip], part_recv.at[a, src_chip], partner)

        def tile_copy(i):
            tile = tile_index(i, core)
            per = block // ROWS
            owner = tile // per
            src = o_tiles.at[:, pl.ds(i * ROWS, ROWS), :]
            dst = o_out.at[:, head, pl.ds(pl.multiple_of((tile % per) * ROWS, ROWS), ROWS), :]
            return owner, pltpu.make_async_copy(src, dst, out_recv), push(src, dst, tile_send.at[i], out_recv, owner)

        def red_copy(a, zi):
            owner = 2 * zi + core
            src, dst = red.at[a, zi], g_out.at[a, head]
            return owner, pltpu.make_async_copy(src, dst, g_recv), push(src, dst, red_send.at[a, zi], g_recv, owner)

        def start(owner, local, remote):
            @pl.when(owner == me)
            def _():
                local.start()

            @pl.when(owner != me)
            def _():
                remote.start()

        def finish(owner, local, remote):
            @pl.when(owner != me)
            def _():
                remote.wait_send()

        for a in range(3):
            for zi in range(n_chips):
                part_copy(a, zi, 1 - core).start()
        for i in range(n_tiles):
            start(*tile_copy(i))
        for a in range(3):
            for zi in range(n_chips):
                part_copy(a, zi, core).wait_recv()
                acc = (dkt, dvt, drt)[a]
                dev = 2 * zi + core
                cols = flip_rows_of(dev) if a == 2 else rows_of(dev)
                total = acc[:, cols] + part[a, zi]
                red[a, zi] = (total if a == 1 else total * scale).astype(BF16)
                start(*red_copy(a, zi))
        for a in range(3):
            for zi in range(n_chips):
                part_copy(a, zi, 1 - core).wait_send()
                finish(*red_copy(a, zi))
        for i in range(n_tiles):
            finish(*tile_copy(i))
        for src in range(n_chips):
            @pl.when(chip != src)
            def _():
                for copy in relay(src):
                    copy.wait_send()
        for copy in relay_own():
            copy.wait_send()

    for dest in range(n_heads):
        @pl.when(chip != dest)
        def _():
            for copy in send_to(dest):
                copy.wait_send()
    pltpu.make_async_copy(o_out, o_out, out_recv).wait()
    pltpu.make_async_copy(g_out, g_out, g_recv).wait()


def group_call(xs, rels, bias, n_dev):
    n_arr, n_heads, block, dim = xs.shape
    seq = block * n_dev
    n_chips = n_dev // 2
    n_tiles = seq // ROWS // 2
    anyw = pl.BlockSpec(memory_space=pl.ANY)
    vmem = pl.BlockSpec(memory_space=pltpu.VMEM)
    dma = pltpu.SemaphoreType.DMA
    return pl.pallas_call(
        group_kernel,
        name='rel_attention',
        in_specs=[anyw, anyw, vmem],
        out_specs=[anyw, anyw, vmem],
        out_shape=[
            jax.ShapeDtypeStruct((2, n_heads, block, dim), BF16),
            jax.ShapeDtypeStruct((3, n_heads, dim, block), BF16),
            jax.ShapeDtypeStruct((8, dim), F32),
        ],
        scratch_shapes=[
            pltpu.VMEM((n_arr, seq, dim), BF16),
            pltpu.VMEM((seq + COLS, dim), BF16),
            pltpu.VMEM((dim, seq), F32),
            pltpu.VMEM((dim, seq), F32),
            pltpu.VMEM((dim, seq + COLS), F32),
            pltpu.VMEM((3, n_chips, dim, block), F32),
            pltpu.VMEM((3, n_chips, dim, block), BF16),
            pltpu.VMEM((2, seq // 2, dim), BF16),
            pltpu.VMEM((ROWS, seq + 2 * ROWS), F32),
            pltpu.VMEM((ROWS, 128), F32),
            pltpu.VMEM((ROWS, 128), F32),
            pltpu.VMEM((ROWS, dim), F32),
            pltpu.VMEM((ROWS, dim), F32),
            pltpu.VMEM((ROWS, dim), F32),
            dma((n_heads, 2)), dma((n_chips, 2)), dma((n_chips, 2)), dma((n_chips, 2)),
            dma((3, n_chips)), dma((3, n_chips)), dma((n_tiles,)), dma((3, n_chips)), dma, dma,
        ],
        compiler_params=pltpu.CompilerParams(vmem_limit_bytes=62 * 2**20, collective_id=0, has_side_effects=True),
    )(xs, rels, bias)


def solution(mesh):
    n_dev = mesh.shape['cp']
    seq_spec = P('cp', 'hp', None)
    head_spec = P('hp', None)
    weight_spec = P(None, 'hp', None)

    def local_fn(q, k, v, u_bias, v_bias, rel_table, w_rel, d_out):
        block, n_heads, dim = q.shape
        rel = jnp.einsum('uo,ojf->juf', rel_table, w_rel, preferred_element_type=F32).astype(BF16)
        xs = jnp.stack([x.transpose(1, 0, 2) for x in (q, k, v, d_out)])
        bias = jnp.pad(jnp.stack([u_bias, v_bias], axis=1), ((0, 0), (0, 6), (0, 0)))
        o, g, bias_acc = group_call(xs, rel[:, ::-1], bias, n_dev)
        chip = lax.axis_index('cp') // 2
        mine = (jnp.arange(n_heads) == chip)[None, :, None]
        d_bias = lax.psum(jnp.where(mine, bias_acc[:2, None, :], 0.0), 'cp')
        d_rel = g[2][:, :, ::-1]
        d_w_rel = lax.psum(jnp.einsum('uo,jfu->ojf', rel_table, d_rel, preferred_element_type=F32), 'cp')
        return (
            o[0].transpose(1, 0, 2),
            o[1].transpose(1, 0, 2),
            g[0].transpose(2, 0, 1),
            g[1].transpose(2, 0, 1),
            d_bias[0],
            d_bias[1],
            d_w_rel,
        )

    return jax.shard_map(
        local_fn,
        mesh=mesh,
        in_specs=(seq_spec, seq_spec, seq_spec, head_spec, head_spec, P('cp', None), weight_spec, seq_spec),
        out_specs=(seq_spec, seq_spec, seq_spec, seq_spec, head_spec, head_spec, weight_spec),
        check_vma=False,
    )
```

time: 3390 us -> 423 us (0.12); the launches traced: 3350 us -> 421 us
  waiting for transfers between devices: 1790 us -> 46.1 us
  starting transfers between devices: 952 us -> 0.04 us
  local copies, waits for them, and re-layouts: 462 us -> 21.6 us
  Pallas kernels: 0 us -> 279 us
  matrix products: 45 us -> 8.17 us
    ppermute x44 -> x0, waiting for transfers between devices: 1440 us -> none  [the longest x7 829 us: bwd_step(): dk_acc = lax.ppermute(dk_acc, 'cp', shift_pairs)]
    ppermute x44 -> x0, starting transfers between devices: 952 us -> none  [the longest x7 321 us: bwd_step(): k_blk = lax.ppermute(k_blk, 'cp', shift_pairs)]
    pallas_call x0 -> x1, Pallas kernels: none -> 279 us  [group_call(): pl.pallas_call(group_kernel, name='rel_attention', in_specs=[anyw, anyw,...]
    reduce_scatter x1 -> x0, waiting for transfers between devices: 275 us -> none  [local_fn(): lax.psum_scatter(grad_rel, 'cp', scatter_dimension=0, tiled=False)]
    cond x56 -> x0, local copies, waits for them, and re-layouts: 151 us -> none
    while x42 -> x0, local copies, waits for them, and re-layouts: 87 us -> none
    reshape x3 -> x0, local copies, waits for them, and re-layouts: 57.1 us -> none  [the longest x2 46.6 us: skew_scores(): kept_view.reshape(lead_dims + (block_len, 2 * block_len - 1))]
    all_gather x1 -> x0, waiting for transfers between devices: 48.6 us -> none  [local_fn(): rel_flipped = lax.all_gather(rel_mine[::-1], 'cp')]
  transfers between devices with their start and end apart: 47 -> 1, of which waited for: 43 -> 1; matrix products, arithmetic and copies ran while one was open for 7% -> 1% of each run, Pallas kernels for 0% -> 0%
where the time goes in v1:
time: 423 us; the launch traced here: 421 us
  Pallas kernels  279 us (66%)
  blocking collectives  50.1 us (12%)
  waiting for transfers between devices  46.1 us (11%)
  local copies, waits for them, and re-layouts  21.6 us (5%)
  between operations  14.1 us (3%)
  matrix products  8.17 us (2%)
    pallas_call x1, Pallas kernels, group_call(): pl.pallas_call(group_kernel, name='rel_attention', in_specs=[anyw, anyw,...  279 us
    psum x1, blocking collectives, local_fn(): d_bias = lax.psum(jnp.where(mine, bias_acc[:2, None, :], 0.0), 'cp')  50.1 us
    psum x1, waiting for transfers between devices, local_fn(): lax.psum(jnp.einsum('uo,jfu->ojf', rel_table, d_rel, preferred_element_ty...  46.1 us
    rev x1, local copies, waits for them, and re-layouts, local_fn(): o, g, bias_acc = group_call(xs, rel[:, ::-1], bias, n_dev)  9.14 us
  transfers between devices with their start and end apart: 1, of which 1 were waited for; matrix products, arithmetic and copies ran while one was open for 1% of the time, Pallas kernels for 0%

profile of v1, /device:TPU:0, one launch (start us, length us, event | category | flops | bytes accessed | tf_op | source)
XLA Modules:
  0.0 421.3 jit_solution(13505242530692304298)
XLA Ops:
  7.2 0.0 copy-start
  7.2 0.0 all-reduce.3.cloned.1.call-start
  7.2 0.8 stack.29
  8.0 0.7 stack.30
  8.7 0.0 copy-done
  8.7 0.0 copy-start.2
  8.7 0.0 copy-start.3
  8.7 0.0 copy-start.4
  8.7 0.0 copy-start.5
  8.7 4.0 fusion.6
  12.7 9.1 %rev.6.rels = bf16[3,768,128]{2,1,0:T(8,128)(2,1)} reverse(bf16[3,768,128]{2,1,0:T(8,128)(2,1)} %fusion.6), dimensions={1} | reverse | bytes 1179648 | tf_op jit(solution)/shard_map/rev | solution.py:336
  21.9 0.6 select_maximum_fusion.bias_ref
  22.5 0.0 copy-done.2
  22.5 0.0 copy-done.3
  22.5 0.0 copy-done.4
  22.5 0.0 copy-done.5
  22.5 1.7 pad_maximum_fusion.xs
  24.2 278.8 %rel_attention.1 = (bf16[2,3,768,128]{3,2,1,0:T(8,128)(2,1)}, bf16[3,3,128,768]{3,2,1,0:T(8,128)(2,1)}, f32[8,128]{1,0:T(8,128)}) custom-call(bf16[4,3,768,128]{3,2,1,0:T(8,128)(2,1)} %pad_maximum_fusion.xs, bf16[3,768,128]{2,1,0:T(8,128)(2,1)} %rev.6.rels, f32[3,8,128]{2,1,0:T(8,128)} %select_maximum_fusion.bias_ref), custom_call_target="tpu_custom_call" | custom-call | tf_op jit(solution)/shard_map/rel_attention/pallas_call | solution.py:293
  303.0 1.5 slice_bitcast_fusion
  304.6 1.8 rev.7
  306.4 4.2 convolution_bitcast_fusion
  310.6 0.0 copy-start.1
  310.6 0.0 all-reduce.3.cloned.1.call-update
  310.6 0.8 slice.28
  311.4 1.1 copy.18
  312.4 1.1 copy.17
  313.5 0.1 broadcast_select_fusion
  313.6 50.1 %psum.14 = f32[2,3,128]{2,1,0:T(4,128)S(1)} all-reduce(f32[2,3,128]{2,1,0:T(4,128)S(1)} %broadcast_select_fusion), channel_id=1, replica_groups=mesh['hp'=4,'cp'=8] {'cp'}, use_global_device_ids=true, to_apply=%region_0.1 | all-reduce | flops 768 | bytes 6144 | tf_op jit(solution)/shard_map/psum | solution.py:339
  363.7 0.6 slice_bitcast_fusion.5
  364.3 0.0 copy-done.1
  364.3 1.1 slice_bitcast_fusion.3
  365.4 46.1 %all-reduce.3.cloned.1.call-done = f32[1536,3,128]{0,2,1:T(8,128)} async-done(((f32[1536,3,128]{0,2,1:T(8,128)}), f32[1536,3,128]{0,2,1:T(8,128)}) %all-reduce.3.cloned.1.call-update) | async-done | bytes 2359312 | tf_op jit(solution)/shard_map/psum | solution.py:341
  411.5 3.0 copy.19
  (1 shorter events, 0.0 us)
Async XLA Ops:
  7.2 1.5 copy-start
  7.2 404.3 %all-reduce.3.cloned.1.call-start = ((), (), s32[]{:S(2)}) async-start(), calls=%async_computation | async-start | bytes 4718592 | tf_op jit(solution)/shard_map/psum | solution.py:341
  8.7 13.8 %copy-start.2 = (bf16[768,3,128]{2,0,1:T(8,128)(2,1)S(1)}, bf16[768,3,128]{2,0,1:T(8,128)(2,1)}, u32[]{:S(2)}) copy-start(bf16[768,3,128]{2,0,1:T(8,128)(2,1)} %param.15) | copy-start | bytes 1769476
  8.7 13.8 %copy-start.3 = (bf16[768,3,128]{2,0,1:T(8,128)(2,1)S(1)}, bf16[768,3,128]{2,0,1:T(8,128)(2,1)}, u32[]{:S(2)}) copy-start(bf16[768,3,128]{2,0,1:T(8,128)(2,1)} %param.10) | copy-start | bytes 1769476
  8.7 13.8 %copy-start.4 = (bf16[768,3,128]{2,0,1:T(8,128)(2,1)S(1)}, bf16[768,3,128]{2,0,1:T(8,128)(2,1)}, u32[]{:S(2)}) copy-start(bf16[768,3,128]{2,0,1:T(8,128)(2,1)} %param.9) | copy-start | bytes 1769476
  8.7 13.8 %copy-start.5 = (bf16[768,3,128]{2,0,1:T(8,128)(2,1)S(1)}, bf16[768,3,128]{2,0,1:T(8,128)(2,1)}, u32[]{:S(2)}) copy-start(bf16[768,3,128]{2,0,1:T(8,128)(2,1)} %param.8) | copy-start | bytes 1769476
  310.6 53.7 %copy-start.1 = (bf16[2,3,768,128]{3,2,1,0:T(8,128)(2,1)S(1)}, bf16[2,3,768,128]{3,2,1,0:T(8,128)(2,1)}, u32[]{:S(2)}) copy-start(bf16[2,3,768,128]{3,2,1,0:T(8,128)(2,1)} %get-tuple-element.10) | copy-start | bytes 3538948
Sparse Core Ops, SparseCore 0:
  310.7 100.6 all-reduce.2

commit v2 on v1

v2 whole, which is shorter than its diff:
```python
import functools
import math

import jax
import jax.numpy as jnp
from jax import lax
from jax.experimental import pallas as pl
from jax.experimental.pallas import tpu as pltpu
from jax.sharding import PartitionSpec as P

F32, BF16 = jnp.float32, jnp.bfloat16
ROWS = 512
COLS = 512
NT = (((1,), (1,)), ((), ()))
NN = (((1,), (0,)), ((), ()))


def mm(a, b, dims=NN, precision=None):
    return lax.dot_general(a, b, dims, preferred_element_type=F32, precision=precision)


def fold_lanes(op, x):
    acc = x[:, :128]
    for g in range(1, x.shape[1] // 128):
        acc = op(acc, x[:, g * 128:(g + 1) * 128])
    return acc


def shear(buf, start, shift):
    out = []
    for g in range(ROWS // 128):
        part = buf[g * 128:(g + 1) * 128, pl.ds(pl.multiple_of(start - (g + 1) * 128, 128), COLS + 128)]
        out.append(pltpu.roll(part, shift, 1, stride=1, stride_axis=0)[:, 128:])
    return jnp.concatenate(out, axis=0)


def flip_rows(anti, x):
    return jnp.concatenate([mm(anti, x[g * 256:(g + 1) * 256]) for g in reversed(range(x.shape[0] // 256))], axis=0)


def tile_grads(q0, out_row, q_ref, k_ref, v_ref, do_ref, rel_ref, bias_ref, o_ref, dq_ref, dkt, dvt, drt, bias_acc, buf, m_ref, l_ref, acc_ref, gu_ref, gv_ref):
    seq, dim = k_ref.shape
    scale = dim ** -0.5
    steps = (q0 + ROWS + COLS - 1) // COLS
    rel0 = seq - ROWS - q0

    def at(base, size):
        return pl.ds(pl.multiple_of(base, 256), size)

    q_wide = q_ref[at(q0, ROWS), :].astype(F32)
    q_u = (q_wide + bias_ref[0:1, :]).astype(BF16)
    q_v = (q_wide + bias_ref[1:2, :]).astype(BF16)

    def offset_scores(c):
        buf[:, at(c * COLS + ROWS, COLS)] = mm(q_v, rel_ref[at(rel0 + c * COLS, COLS), :], NT)

    def scores(c):
        j0 = c * COLS
        return mm(q_u, k_ref[at(j0, COLS), :], NT) + shear(buf, j0 + 2 * ROWS, 1)

    def keep(c, score):
        buf[:, at(c * COLS + ROWS, COLS)] = score
        m_ref[...] = jnp.maximum(m_ref[...], fold_lanes(jnp.maximum, score))

    m_ref[...] = jnp.full_like(m_ref, -jnp.inf)
    offset_scores(0)

    @pl.loop(0, steps - 1)
    def _(c):
        offset_scores(c + 1)
        keep(c, scores(c))

    row_minus_col = lax.broadcasted_iota(jnp.int32, (ROWS, COLS), 0) - lax.broadcasted_iota(jnp.int32, (ROWS, COLS), 1)
    last = steps - 1
    keep(last, jnp.where(row_minus_col >= last * COLS - q0, scores(last), -jnp.inf))

    row_max = jnp.max(m_ref[...], axis=1, keepdims=True)
    l_ref[...] = jnp.zeros_like(l_ref)
    acc_ref[...] = jnp.zeros_like(acc_ref)

    @pl.loop(0, steps)
    def _(c):
        j0 = c * COLS
        prob = jnp.exp2((buf[:, at(j0 + ROWS, COLS)] - row_max) * (scale * math.log2(math.e)))
        buf[:, at(j0 + ROWS, COLS)] = prob
        l_ref[...] += fold_lanes(jnp.add, prob)
        acc_ref[...] += mm(prob.astype(BF16), v_ref[at(j0, COLS), :])

    inv_sum = 1.0 / jnp.sum(l_ref[...], axis=1, keepdims=True)
    out = acc_ref[...] * inv_sum
    o_ref[at(out_row, ROWS), :] = out.astype(BF16)
    d_out = do_ref[at(q0, ROWS), :]
    do_wide = d_out.astype(F32)
    delta = jnp.sum(do_wide * out, axis=1, keepdims=True)
    anti = (lax.broadcasted_iota(jnp.int32, (256, 256), 0) + lax.broadcasted_iota(jnp.int32, (256, 256), 1) == 255)
    anti_b = anti.astype(F32).astype(BF16)
    do_t = do_wide.T.astype(BF16)
    qu_t = q_u.astype(F32).T.astype(BF16)
    qv_rt = flip_rows(anti_b, q_v).T.astype(BF16)
    gu_ref[...] = jnp.zeros_like(gu_ref)
    gv_ref[...] = jnp.zeros_like(gv_ref)

    def by_key(c):
        j0 = c * COLS
        cols = at(j0, COLS)
        prob = buf[:, at(j0 + ROWS, COLS)] * inv_sum
        ds = (prob * (mm(d_out, v_ref[cols, :], NT) - delta)).astype(BF16)
        dvt[:, cols] += mm(do_t, prob.astype(BF16))
        dkt[:, cols] += mm(qu_t, ds)
        gu_ref[...] += mm(ds, k_ref[cols, :])
        buf[:, at(j0 + ROWS, COLS)] = flip_rows(anti_b, ds)

    def by_offset(c):
        c0 = c * COLS
        ds = shear(buf, c0 + ROWS, 0).astype(BF16)
        cols = at(rel0 + c0, COLS)
        gv_ref[...] += mm(ds, rel_ref[cols, :])
        drt[:, cols] += mm(qv_rt, ds)

    by_key(0)

    @pl.loop(1, steps)
    def _(c):
        by_offset(c - 1)
        by_key(c)

    by_offset(steps - 1)

    g_u = gu_ref[...]
    g_vr = gv_ref[...]
    anti_f = anti.astype(F32)
    g_v = jnp.concatenate([mm(anti_f, g_vr[g * 256:(g + 1) * 256], precision=lax.Precision.HIGHEST) for g in reversed(range(ROWS // 256))], axis=0)
    dq_ref[at(out_row, ROWS), :] = ((g_u + g_v) * scale).astype(BF16)
    bias_acc[0:1, :] += jnp.sum(g_u, axis=0, keepdims=True) * scale
    bias_acc[1:2, :] += jnp.sum(g_vr, axis=0, keepdims=True) * scale


def tile_index(i, core):
    return 4 * (i // 2) + jnp.where(i % 2 == 0, core, 3 - core)


def group_kernel(xs, rels, bias_ref, o_out, g_out, bias_out, xh, relh, rel_flip, dkt, dvt, drt, part, red, o_tiles, bias_acc, bias_in, *rest):
    scratch, sems = rest[:6], rest[6:]
    in_send, in_recv, fwd_send, fwd_recv, part_send, part_recv, tile_send, red_send, bias_send, out_recv, g_recv, bias_recv = sems
    n_arr, n_heads, block, dim = xs.shape
    n_dev = lax.axis_size('cp')
    n_chips = n_dev // 2
    seq = block * n_dev
    scale = dim ** -0.5
    me = lax.axis_index('cp')
    chip, core = me // 2, me % 2
    head = jnp.minimum(chip, n_heads - 1)
    active = chip < n_heads
    partner = 2 * chip + 1 - core
    n_tiles = seq // ROWS // 2

    barrier = pltpu.get_barrier_semaphore()
    for d in range(1, n_dev):
        pl.semaphore_signal(barrier, inc=1, device_id={'cp': (me + d) % n_dev}, device_id_type=pl.DeviceIdType.MESH)
    pl.semaphore_wait(barrier, n_dev - 1)

    def push(src, dst, send, recv, dev):
        return pltpu.make_async_remote_copy(src_ref=src, dst_ref=dst, send_sem=send, recv_sem=recv, device_id={'cp': dev}, device_id_type=pl.DeviceIdType.MESH)

    def rows_of(dev):
        return pl.ds(pl.multiple_of(dev * block, block), block)

    def flip_rows_of(dev):
        return pl.ds(pl.multiple_of(seq - block - dev * block, block), block)

    def x_copy(dest, src_dev, src, send, recv, dev):
        return push(src, xh.at[:, rows_of(src_dev), :], send.at[0], recv.at[0], dev)

    def rel_copy(dest, src_dev, src, send, recv, dev):
        return push(src, relh.at[flip_rows_of(src_dev), :], send.at[1], recv.at[1], dev)

    def to_head(make, srcs, dest):
        return make(dest, me, srcs, in_send.at[dest], in_recv.at[chip], 2 * dest + core)

    def x_to_head(dest):
        return to_head(x_copy, xs.at[:, dest], dest)

    def rel_to_head(dest):
        return to_head(rel_copy, rel_flip.at[dest], dest)

    def x_to_partner(dev, src, recv_dev):
        return x_copy(head, dev, src, fwd_send.at[dev // 2], fwd_recv.at[dev // 2], recv_dev)

    def rel_to_partner(dev, src, recv_dev):
        return rel_copy(head, dev, src, fwd_send.at[dev // 2], fwd_recv.at[dev // 2], recv_dev)

    def x_local():
        return pltpu.make_async_copy(xs.at[:, head], xh.at[:, rows_of(me), :], in_recv.at[chip, 0])

    def rel_local():
        return pltpu.make_async_copy(rel_flip.at[head], relh.at[flip_rows_of(me), :], in_recv.at[chip, 1])

    anti = (lax.broadcasted_iota(jnp.int32, (256, 256), 0) + lax.broadcasted_iota(jnp.int32, (256, 256), 1) == 255).astype(F32).astype(BF16)
    orders = ((1, 2), (2, 0), (0, 1), (2, 0, 1))
    for z, order in enumerate(orders):
        @pl.when(chip == z)
        def _():
            for dest in order:
                if dest != z:
                    x_to_head(dest).start()

    @pl.when(active)
    def _():
        x_local().start()
        x_to_partner(me, xs.at[:, head], partner).start()

    for h in range(n_heads):
        rel_flip[h] = flip_rows(anti, rels[h]).astype(BF16)

    for z, order in enumerate(orders):
        @pl.when(chip == z)
        def _():
            for dest in order:
                if dest != z:
                    rel_to_head(dest).start()

    @pl.when(active)
    def _():
        rel_local().start()
        rel_to_partner(me, rel_flip.at[head], partner).start()

    dkt[...] = jnp.zeros_like(dkt)
    dvt[...] = jnp.zeros_like(dvt)
    drt[...] = jnp.zeros_like(drt)
    bias_acc[...] = jnp.zeros_like(bias_acc)
    scratch[0][:, :ROWS] = jnp.zeros((ROWS, ROWS), F32)
    relh[pl.ds(seq, COLS), :] = jnp.zeros((COLS, dim), BF16)

    q_ref, k_ref, v_ref, do_ref = (xh.at[a] for a in range(4))
    pieces = ROWS // 256

    def start(owner, local, remote):
        @pl.when(owner == me)
        def _():
            local().start()

        @pl.when(owner != me)
        def _():
            remote().start()

    def finish(owner, local, remote):
        @pl.when(owner != me)
        def _():
            remote().wait_send()

    def tile_copy(i, g):
        piece = tile_index(i, core) * pieces + g
        per = block // 256
        owner = piece // per
        src = o_tiles.at[:, pl.ds(pl.multiple_of(i * ROWS + g * 256, 256), 256), :]
        dst = o_out.at[:, head, pl.ds(pl.multiple_of((piece % per) * 256, 256), 256), :]
        return owner, lambda: pltpu.make_async_copy(src, dst, out_recv), lambda: push(src, dst, tile_send.at[i, g], out_recv, owner)

    def ready_blocks(i):
        return (2 * ROWS * i + block - 1) // block

    @pl.when(active)
    def _():
        @pl.loop(0, n_tiles)
        def _(i):
            @pl.loop(ready_blocks(i), ready_blocks(i + 1))
            def _(dev):
                @pl.when(dev == me)
                def _():
                    x_local().wait()
                    rel_local().wait()

                @pl.when((dev % 2 == core) & (dev != me))
                def _():
                    x_copy(head, dev, xs.at[:, head], in_send.at[0], in_recv.at[dev // 2], partner).wait_recv()
                    rel_copy(head, dev, rel_flip.at[head], in_send.at[0], in_recv.at[dev // 2], partner).wait_recv()
                    x_to_partner(dev, xh.at[:, rows_of(dev), :], partner).start()
                    rel_to_partner(dev, relh.at[flip_rows_of(dev), :], partner).start()

            @pl.loop(ready_blocks(i), ready_blocks(i + 1))
            def _(dev):
                @pl.when(dev % 2 != core)
                def _():
                    x_to_partner(dev, xs.at[:, head], partner).wait_recv()
                    rel_to_partner(dev, rel_flip.at[head], partner).wait_recv()

            tile_grads(tile_index(i, core) * ROWS, i * ROWS, q_ref, k_ref, v_ref, do_ref, relh, bias_ref.at[head], o_tiles.at[0], o_tiles.at[1], dkt, dvt, drt, bias_acc, *scratch)
            for g in range(pieces):
                start(*tile_copy(i, g))

        def acc_cols(a, dev):
            return (dkt, dvt, drt)[a], flip_rows_of(dev) if a == 2 else rows_of(dev)

        def part_copy(a, src_chip, parity):
            acc, cols = acc_cols(a, 2 * src_chip + parity)
            return push(acc.at[:, cols], part.at[a, src_chip], part_send.at[a, src_chip], part_recv.at[a, src_chip], partner)

        def red_copy(a, zi):
            owner = 2 * zi + core
            src, dst = red.at[a, zi], g_out.at[a, head]
            return owner, lambda: pltpu.make_async_copy(src, dst, g_recv), lambda: push(src, dst, red_send.at[a, zi], g_recv, owner)

        def bias_copy(d):
            owner = (me + d) % n_dev
            src, dst = bias_acc, bias_in.at[2 * head + core]
            return owner, lambda: pltpu.make_async_copy(src, dst, bias_recv), lambda: push(src, dst, bias_send.at[d], bias_recv, owner)

        arrays = (2, 0, 1)
        for a in arrays:
            for zi in range(n_chips):
                part_copy(a, zi, 1 - core).start()
        for d in range(n_dev):
            start(*bias_copy(d))
        for a in arrays:
            for zi in range(n_chips):
                part_copy(a, zi, core).wait_recv()
                acc, cols = acc_cols(a, 2 * zi + core)
                total = acc[:, cols] + part[a, zi]
                red[a, zi] = (total if a == 1 else total * scale).astype(BF16)
                start(*red_copy(a, zi))
        for a in arrays:
            for zi in range(n_chips):
                part_copy(a, zi, 1 - core).wait_send()
                finish(*red_copy(a, zi))
        for d in range(n_dev):
            finish(*bias_copy(d))

        @pl.loop(0, n_tiles)
        def _(i):
            for g in range(pieces):
                finish(*tile_copy(i, g))

        @pl.loop(0, n_chips)
        def _(z):
            x_to_partner(2 * z + core, xs.at[:, head], partner).wait_send()
            rel_to_partner(2 * z + core, rel_flip.at[head], partner).wait_send()

    for dest in range(n_heads):
        @pl.when(chip != dest)
        def _():
            x_to_head(dest).wait_send()
            rel_to_head(dest).wait_send()
    pltpu.make_async_copy(bias_in, bias_in, bias_recv).wait()
    for h in range(n_heads):
        bias_out[h] = bias_in[2 * h] + bias_in[2 * h + 1]
    pltpu.make_async_copy(o_out, o_out, out_recv).wait()
    pltpu.make_async_copy(g_out, g_out, g_recv).wait()


def group_call(xs, rels, bias, n_dev):
    n_arr, n_heads, block, dim = xs.shape
    seq = block * n_dev
    n_chips = n_dev // 2
    n_tiles = seq // ROWS // 2
    anyw = pl.BlockSpec(memory_space=pl.ANY)
    vmem = pl.BlockSpec(memory_space=pltpu.VMEM)
    dma = pltpu.SemaphoreType.DMA
    return pl.pallas_call(
        group_kernel,
        name='rel_attention',
        in_specs=[anyw, vmem, vmem],
        out_specs=[anyw, anyw, vmem],
        out_shape=[
            jax.ShapeDtypeStruct((2, n_heads, block, dim), BF16),
            jax.ShapeDtypeStruct((3, n_heads, dim, block), BF16),
            jax.ShapeDtypeStruct((n_heads, 8, dim), F32),
        ],
        scratch_shapes=[
            pltpu.VMEM((n_arr, seq, dim), BF16),
            pltpu.VMEM((seq + COLS, dim), BF16),
            pltpu.VMEM((n_heads, block, dim), BF16),
            pltpu.VMEM((dim, seq), F32),
            pltpu.VMEM((dim, seq), F32),
            pltpu.VMEM((dim, seq + COLS), F32),
            pltpu.VMEM((3, n_chips, dim, block), F32),
            pltpu.VMEM((3, n_chips, dim, block), BF16),
            pltpu.VMEM((2, seq // 2, dim), BF16),
            pltpu.VMEM((8, dim), F32),
            pltpu.VMEM((2 * n_heads, 8, dim), F32),
            pltpu.VMEM((ROWS, seq + ROWS + COLS), F32),
            pltpu.VMEM((ROWS, 128), F32),
            pltpu.VMEM((ROWS, 128), F32),
            pltpu.VMEM((ROWS, dim), F32),
            pltpu.VMEM((ROWS, dim), F32),
            pltpu.VMEM((ROWS, dim), F32),
            dma((n_heads, 2)), dma((n_chips, 2)), dma((n_chips, 2)), dma((n_chips, 2)),
            dma((3, n_chips)), dma((3, n_chips)), dma((n_tiles, ROWS // 256)), dma((3, n_chips)), dma((n_dev,)), dma, dma, dma,
        ],
        compiler_params=pltpu.CompilerParams(vmem_limit_bytes=63 * 2**20, collective_id=0, has_side_effects=True),
    )(xs, rels, bias)


def solution(mesh):
    n_dev = mesh.shape['cp']
    seq_spec = P('cp', 'hp', None)
    head_spec = P('hp', None)
    weight_spec = P(None, 'hp', None)

    def local_fn(q, k, v, u_bias, v_bias, rel_table, w_rel, d_out):
        block, n_heads, dim = q.shape
        rel = jnp.einsum('uo,ojf->juf', rel_table, w_rel, preferred_element_type=F32).astype(BF16)
        xs = jnp.stack([x.transpose(1, 0, 2) for x in (q, k, v, d_out)])
        bias = jnp.pad(jnp.stack([u_bias, v_bias], axis=1), ((0, 0), (0, 6), (0, 0)))
        o, g, d_bias = group_call(xs, rel, bias, n_dev)
        d_rel = g[2][:, :, ::-1]
        d_w_rel = lax.psum(jnp.einsum('uo,jfu->ojf', rel_table, d_rel, preferred_element_type=F32), 'cp')
        return (
            o[0].transpose(1, 0, 2),
            o[1].transpose(1, 0, 2),
            g[0].transpose(2, 0, 1),
            g[1].transpose(2, 0, 1),
            d_bias[:, 0],
            d_bias[:, 1],
            d_w_rel,
        )

    return jax.shard_map(
        local_fn,
        mesh=mesh,
        in_specs=(seq_spec, seq_spec, seq_spec, head_spec, head_spec, P('cp', None), weight_spec, seq_spec),
        out_specs=(seq_spec, seq_spec, seq_spec, seq_spec, head_spec, head_spec, weight_spec),
        check_vma=False,
    )
```

time: 423 us -> 324 us (0.77)
  Pallas kernels: 279 us -> 206 us
  blocking collectives: 50.1 us -> 0 us
  waiting for transfers between devices: 46.1 us -> 80.4 us
  local copies, waits for them, and re-layouts: 21.6 us -> 12.4 us
    pallas_call x1, Pallas kernels: 279 us -> 206 us  [group_call(): pl.pallas_call(group_kernel, name='rel_attention', in_specs=[anyw, vmem,...]
    psum x1 -> x0, blocking collectives: 50.1 us -> none  [local_fn(): d_bias = lax.psum(jnp.where(mine, bias_acc[:2, None, :], 0.0), 'cp')]
    psum x1, waiting for transfers between devices: 46.1 us -> 80.4 us  [local_fn(): lax.psum(jnp.einsum('uo,jfu->ojf', rel_table, d_rel, preferred_element_ty...]
    rev x1 -> x0, local copies, waits for them, and re-layouts: 9.14 us -> none  [local_fn(): o, g, bias_acc = group_call(xs, rel[:, ::-1], bias, n_dev)]
where the time goes in v2:
time: 324 us
  Pallas kernels  206 us (64%)
  waiting for transfers between devices  80.4 us (25%)
  between operations  14.1 us (4%)
  local copies, waits for them, and re-layouts  12.4 us (4%)
  matrix products  8.48 us (3%)
    pallas_call x1, Pallas kernels, group_call(): pl.pallas_call(group_kernel, name='rel_attention', in_specs=[anyw, vmem,...  206 us
    psum x1, waiting for transfers between devices, local_fn(): lax.psum(jnp.einsum('uo,jfu->ojf', rel_table, d_rel, preferred_element_ty...  80.4 us
  transfers between devices with their start and end apart: 1, of which 1 were waited for; matrix products, arithmetic and copies ran while one was open for 1% of the time, Pallas kernels for 0%

profile of v2, /device:TPU:0, one launch (start us, length us, event | category | flops | bytes accessed | tf_op | source)
XLA Modules:
  0.0 323.7 jit_solution(5607890687350873665)
XLA Ops:
  7.2 0.0 all-reduce.3.cloned.1.call-start
  7.2 0.7 stack.29
  7.9 0.7 stack.30
  8.6 0.6 select_maximum_fusion.bias_ref
  9.2 0.0 copy-start.1
  9.2 0.0 copy-start.2
  9.2 0.0 copy-start.3
  9.2 0.0 copy-start.4
  9.2 4.3 %fusion.6.rels = bf16[3,768,128]{2,1,0:T(8,128)(2,1)} fusion(bf16[1536,3,128]{2,0,1:T(8,128)(2,1)} %param.14, bf16[768,1536]{1,0:T(8,128)(2,1)} %param.13), kind=kOutput, calls=%fused_computation.6 | convolution fusion | flops 906264576 | bytes 4128768 | tf_op jit(solution)/shard_map/uo,ojf->juf/dot_general | solution.py:401
  13.5 0.0 copy-done.1
  13.5 0.0 copy-done.2
  13.5 0.0 copy-done.3
  13.5 0.0 copy-done.4
  13.6 1.7 pad_maximum_fusion.xs
  15.3 205.9 %rel_attention.1 = (bf16[2,3,768,128]{3,2,1,0:T(8,128)(2,1)}, bf16[3,3,128,768]{3,2,1,0:T(8,128)(2,1)}, f32[3,8,128]{2,1,0:T(8,128)}) custom-call(bf16[4,3,768,128]{3,2,1,0:T(8,128)(2,1)} %pad_maximum_fusion.xs, bf16[3,768,128]{2,1,0:T(8,128)(2,1)} %fusion.6.rels, f32[3,8,128]{2,1,0:T(8,128)} %select_maximum_fusion.bias_ref), custom_call_target="tpu_custom_call" | custom-call | tf_op jit(solution)/shard_map/rel_attention/pallas_call | solution.py:358
  221.2 1.5 slice_bitcast_fusion
  222.8 1.8 rev.3
  224.6 4.2 %convolution_bitcast_fusion = f32[1536,3,128]{0,2,1:T(8,128)} fusion(bf16[3,128,768]{2,1,0:T(8,128)(2,1)S(1)} %rev.3, bf16[768,1536]{1,0:T(8,128)(2,1)} %param.13), kind=kOutput, calls=%fused_computation | convolution fusion | flops 905969664 | bytes 5308416 | tf_op jit(solution)/shard_map/uo,jfu->ojf/dot_general | solution.py:406
  228.8 0.0 copy-start
  228.8 0.0 all-reduce.3.cloned.1.call-update
  228.8 1.1 copy.18
  229.8 1.1 copy.17
  230.9 0.8 fusion.9
  231.7 0.6 copy_bitcast_fusion
  232.3 0.0 copy-done
  232.3 1.1 slice_bitcast_fusion.3
  233.4 80.4 %all-reduce.3.cloned.1.call-done = f32[1536,3,128]{0,2,1:T(8,128)} async-done(((f32[1536,3,128]{0,2,1:T(8,128)}), f32[1536,3,128]{0,2,1:T(8,128)}) %all-reduce.3.cloned.1.call-update) | async-done | bytes 2359312 | tf_op jit(solution)/shard_map/psum | solution.py:406
  313.8 3.0 copy.19
Async XLA Ops:
  7.2 306.6 %all-reduce.3.cloned.1.call-start = ((), (), s32[]{:S(2)}) async-start(), calls=%async_computation | async-start | bytes 4718592 | tf_op jit(solution)/shard_map/psum | solution.py:406
  9.2 4.3 %copy-start.1 = (bf16[768,3,128]{2,0,1:T(8,128)(2,1)S(1)}, bf16[768,3,128]{2,0,1:T(8,128)(2,1)}, u32[]{:S(2)}) copy-start(bf16[768,3,128]{2,0,1:T(8,128)(2,1)} %param.15) | copy-start | bytes 1769476
  9.2 4.3 %copy-start.2 = (bf16[768,3,128]{2,0,1:T(8,128)(2,1)S(1)}, bf16[768,3,128]{2,0,1:T(8,128)(2,1)}, u32[]{:S(2)}) copy-start(bf16[768,3,128]{2,0,1:T(8,128)(2,1)} %param.10) | copy-start | bytes 1769476
  9.2 4.3 %copy-start.3 = (bf16[768,3,128]{2,0,1:T(8,128)(2,1)S(1)}, bf16[768,3,128]{2,0,1:T(8,128)(2,1)}, u32[]{:S(2)}) copy-start(bf16[768,3,128]{2,0,1:T(8,128)(2,1)} %param.9) | copy-start | bytes 1769476
  9.2 4.3 %copy-start.4 = (bf16[768,3,128]{2,0,1:T(8,128)(2,1)S(1)}, bf16[768,3,128]{2,0,1:T(8,128)(2,1)}, u32[]{:S(2)}) copy-start(bf16[768,3,128]{2,0,1:T(8,128)(2,1)} %param.8) | copy-start | bytes 1769476
  228.8 3.5 %copy-start = (bf16[2,3,768,128]{3,2,1,0:T(8,128)(2,1)S(1)}, bf16[2,3,768,128]{3,2,1,0:T(8,128)(2,1)}, u32[]{:S(2)}) copy-start(bf16[2,3,768,128]{3,2,1,0:T(8,128)(2,1)} %get-tuple-element.10) | copy-start | bytes 3538948
Sparse Core Ops, SparseCore 0:
  228.9 84.8 all-reduce.2

commit v3 on v2

--- a/solution.py
+++ b/solution.py
@@ -11,6 +11,7 @@
 F32, BF16 = jnp.float32, jnp.bfloat16
 ROWS = 512
 COLS = 512
+SUBS = 4
 NT = (((1,), (1,)), ((), ()))
 NN = (((1,), (0,)), ((), ()))
 
@@ -38,7 +39,7 @@
     return jnp.concatenate([mm(anti, x[g * 256:(g + 1) * 256]) for g in reversed(range(x.shape[0] // 256))], axis=0)
 
 
-def tile_grads(q0, out_row, q_ref, k_ref, v_ref, do_ref, rel_ref, bias_ref, o_ref, dq_ref, dkt, dvt, drt, bias_acc, buf, m_ref, l_ref, acc_ref, gu_ref, gv_ref):
+def tile_grads(q0, out_row, q_ref, k_ref, v_ref, do_ref, rel_ref, bias_ref, o_ref, dq_ref, dkt, dvt, drt, bias_acc, buf, m_ref, l_ref, acc_ref, gu_ref, gv_ref, after_step=None):
     seq, dim = k_ref.shape
     scale = dim ** -0.5
     steps = (q0 + ROWS + COLS - 1) // COLS
@@ -123,8 +124,14 @@
     def _(c):
         by_offset(c - 1)
         by_key(c)
+        if after_step is not None:
+            after_step(c - 1)
 
     by_offset(steps - 1)
+    if after_step is not None:
+        @pl.loop(steps - 1, seq // COLS)
+        def _(c):
+            after_step(c)
 
     g_u = gu_ref[...]
     g_vr = gv_ref[...]
@@ -139,13 +146,15 @@
     return 4 * (i // 2) + jnp.where(i % 2 == 0, core, 3 - core)
 
 
-def group_kernel(xs, rels, bias_ref, o_out, g_out, bias_out, xh, relh, rel_flip, dkt, dvt, drt, part, red, o_tiles, bias_acc, bias_in, *rest):
+def group_kernel(xs, rt_hbm, w_hbm, bias_ref, o_out, g_out, bias_out, w_out, xh, relh, rel_flip, rt, w2, dkt, dvt, drt, part, red, o_tiles, bias_acc, bias_in, dr_in, w_part, w_in, rs_in, *rest):
     scratch, sems = rest[:6], rest[6:]
-    in_send, in_recv, fwd_send, fwd_recv, part_send, part_recv, tile_send, red_send, bias_send, out_recv, g_recv, bias_recv = sems
+    (in_send, in_recv, fwd_send, fwd_recv, part_send, part_recv, tile_send, red_send, bias_send, out_recv, g_recv, bias_recv, load_sem,
+     dr_recv, pair_send, pair_recv, rs_send, rs_recv, ag_send, ag_recv, agp_recv) = sems
     n_arr, n_heads, block, dim = xs.shape
     n_dev = lax.axis_size('cp')
     n_chips = n_dev // 2
     seq = block * n_dev
+    n_steps = seq // COLS
     scale = dim ** -0.5
     me = lax.axis_index('cp')
     chip, core = me // 2, me % 2
@@ -154,6 +163,11 @@
     partner = 2 * chip + 1 - core
     n_tiles = seq // ROWS // 2
 
+    load_rt = pltpu.make_async_copy(rt_hbm, rt, load_sem.at[0])
+    load_w = pltpu.make_async_copy(w_hbm, w2, load_sem.at[1])
+    load_rt.start()
+    load_w.start()
+
     barrier = pltpu.get_barrier_semaphore()
     for d in range(1, n_dev):
         pl.semaphore_signal(barrier, inc=1, device_id={'cp': (me + d) % n_dev}, device_id_type=pl.DeviceIdType.MESH)
@@ -209,8 +223,17 @@
         x_local().start()
         x_to_partner(me, xs.at[:, head], partner).start()
 
-    for h in range(n_heads):
-        rel_flip[h] = flip_rows(anti, rels[h]).astype(BF16)
+    load_rt.wait()
+    load_w.wait()
+    n_groups = block // 256
+
+    @pl.loop(0, n_groups)
+    def _(g):
+        rows = pl.ds(pl.multiple_of(g * 256, 256), 256)
+        flipped = pl.ds(pl.multiple_of((n_groups - 1 - g) * 256, 256), 256)
+        rel = mm(anti, mm(rt[rows, :], w2[...]).astype(BF16)).astype(BF16)
+        for h in range(n_heads):
+            rel_flip[h, flipped, :] = rel[:, h * dim:(h + 1) * dim]
 
     for z, order in enumerate(orders):
         @pl.when(chip == z)
@@ -248,21 +271,61 @@
         def _():
             remote().wait_send()
 
+    per = block // 256
+
+    def piece_of(g):
+        return pl.ds(pl.multiple_of(g * 256, 256), 256)
+
     def tile_copy(i, g):
         piece = tile_index(i, core) * pieces + g
-        per = block // 256
         owner = piece // per
-        src = o_tiles.at[:, pl.ds(pl.multiple_of(i * ROWS + g * 256, 256), 256), :]
-        dst = o_out.at[:, head, pl.ds(pl.multiple_of((piece % per) * 256, 256), 256), :]
+        src = o_tiles.at[:, piece_of(i * pieces + g), :]
+        dst = o_out.at[:, head, piece_of(piece % per), :]
         return owner, lambda: pltpu.make_async_copy(src, dst, out_recv), lambda: push(src, dst, tile_send.at[i, g], out_recv, owner)
 
     def ready_blocks(i):
         return (2 * ROWS * i + block - 1) // block
 
+    accs = (dkt, dvt, drt)
+    arrays = (2, 0, 1)
+
+    def part_copy(a, c, parity):
+        return push(accs[a].at[:, piece_of(2 * c + parity)], part.at[a, c], part_send.at[a, c], part_recv.at[a, c], partner)
+
+    def red_copy(a, c):
+        piece = 2 * c + core
+        if a == 2:
+            owner, dst, recv = n_dev - 1 - piece // per, dr_in.at[head, :, piece_of(piece % per)], dr_recv
+        else:
+            owner, dst, recv = piece // per, g_out.at[a, head, :, piece_of(piece % per)], g_recv
+        src = red.at[a, c]
+        return owner, lambda: pltpu.make_async_copy(src, dst, recv), lambda: push(src, dst, red_send.at[a, c], recv, owner)
+
+    def reduce(c):
+        for a in arrays:
+            part_copy(a, c, core).wait_recv()
+            total = accs[a][:, piece_of(2 * c + core)] + part[a, c]
+            red[a, c] = (total if a == 1 else total * scale).astype(BF16)
+            start(*red_copy(a, c))
+
+    lag = 2
+
+    def after_step(c):
+        for a in arrays:
+            part_copy(a, c, 1 - core).start()
+
+        @pl.when(c >= lag)
+        def _():
+            reduce(c - lag)
+
+    def bias_copy(d):
+        owner = (me + d) % n_dev
+        src, dst = bias_acc, bias_in.at[2 * head + core]
+        return owner, lambda: pltpu.make_async_copy(src, dst, bias_recv), lambda: push(src, dst, bias_send.at[d], bias_recv, owner)
+
     @pl.when(active)
     def _():
-        @pl.loop(0, n_tiles)
-        def _(i):
+        def tile(i, **kw):
             @pl.loop(ready_blocks(i), ready_blocks(i + 1))
             def _(dev):
                 @pl.when(dev == me)
@@ -284,44 +347,154 @@
                     x_to_partner(dev, xs.at[:, head], partner).wait_recv()
                     rel_to_partner(dev, rel_flip.at[head], partner).wait_recv()
 
-            tile_grads(tile_index(i, core) * ROWS, i * ROWS, q_ref, k_ref, v_ref, do_ref, relh, bias_ref.at[head], o_tiles.at[0], o_tiles.at[1], dkt, dvt, drt, bias_acc, *scratch)
+            tile_grads(tile_index(i, core) * ROWS, i * ROWS, q_ref, k_ref, v_ref, do_ref, relh, bias_ref.at[head], o_tiles.at[0], o_tiles.at[1], dkt, dvt, drt, bias_acc, *scratch, **kw)
             for g in range(pieces):
                 start(*tile_copy(i, g))
 
-        def acc_cols(a, dev):
-            return (dkt, dvt, drt)[a], flip_rows_of(dev) if a == 2 else rows_of(dev)
-
-        def part_copy(a, src_chip, parity):
-            acc, cols = acc_cols(a, 2 * src_chip + parity)
-            return push(acc.at[:, cols], part.at[a, src_chip], part_send.at[a, src_chip], part_recv.at[a, src_chip], partner)
-
-        def red_copy(a, zi):
-            owner = 2 * zi + core
-            src, dst = red.at[a, zi], g_out.at[a, head]
-            return owner, lambda: pltpu.make_async_copy(src, dst, g_recv), lambda: push(src, dst, red_send.at[a, zi], g_recv, owner)
-
-        def bias_copy(d):
-            owner = (me + d) % n_dev
-            src, dst = bias_acc, bias_in.at[2 * head + core]
-            return owner, lambda: pltpu.make_async_copy(src, dst, bias_recv), lambda: push(src, dst, bias_send.at[d], bias_recv, owner)
-
-        arrays = (2, 0, 1)
-        for a in arrays:
-            for zi in range(n_chips):
-                part_copy(a, zi, 1 - core).start()
+        @pl.loop(0, n_tiles - 1)
+        def _(i):
+            tile(i)
+
+        tile(jnp.int32(n_tiles - 1), after_step=after_step)
+
         for d in range(n_dev):
             start(*bias_copy(d))
-        for a in arrays:
-            for zi in range(n_chips):
-                part_copy(a, zi, core).wait_recv()
-                acc, cols = acc_cols(a, 2 * zi + core)
-                total = acc[:, cols] + part[a, zi]
-                red[a, zi] = (total if a == 1 else total * scale).astype(BF16)
-                start(*red_copy(a, zi))
-        for a in arrays:
-            for zi in range(n_chips):
-                part_copy(a, zi, 1 - core).wait_send()
-                finish(*red_copy(a, zi))
+
+        @pl.loop(n_steps - lag, n_steps)
+        def _(c):
+            reduce(c)
+
+    half, quarter = w_part.shape[0] // 2, w_part.shape[0] // 2 // n_chips
+    sub = quarter // SUBS
+    pltpu.make_async_copy(dr_in, dr_in, dr_recv).wait()
+
+    def d_rel_of(h):
+        return jnp.concatenate([mm(dr_in[h, :, g * 256:(g + 1) * 256], anti) for g in reversed(range(n_groups))], axis=1).astype(BF16)
+
+    d_rel = jnp.concatenate([d_rel_of(h) for h in range(n_heads)], axis=0)
+
+    def half_rows(c):
+        return pl.ds(pl.multiple_of(c * half, half), half)
+
+    def w_rows(c):
+        @pl.loop(0, half // 256)
+        def _(g):
+            rows = pl.ds(pl.multiple_of(c * half + g * 256, 256), 256)
+            w_part[rows, :] = lax.dot_general(rt[:, rows], d_rel, (((0,), (1,)), ((), ())), preferred_element_type=F32)
+
+    pair = push(w_part.at[half_rows(1 - core), :], w_in, pair_send, pair_recv, partner)
+    w_rows(1 - core)
+    pair.start()
+    w_rows(core)
+    pair.wait_recv()
+
+    def sub_rows(q, s):
+        return pl.ds(pl.multiple_of(core * half + q * quarter + s * sub, 8), sub)
+
+    def in_rows(q, s):
+        return pl.ds(pl.multiple_of(q * quarter + s * sub, 8), sub)
+
+    def rs_copy(side, q, s):
+        dev = 2 * (chip + (1 if side == 0 else -1)) + core
+        dev = jnp.clip(dev, 0, n_dev - 1)
+        return push(w_part.at[sub_rows(q, s), :], rs_in.at[side, in_rows(q, s), :], rs_send.at[side, q, s], rs_recv.at[side, q, s], dev)
+
+    def ag_copy(way, q, s):
+        dev = (2 * (chip + 1) + core, 2 * (chip - 1) + core, partner)[way]
+        dev = jnp.clip(dev, 0, n_dev - 1)
+        rows = sub_rows(q, s)
+        return push(w_out.at[rows, :], w_out.at[rows, :], ag_send.at[way, q, s], agp_recv if way == 2 else ag_recv.at[q, s], dev)
+
+    def flow(side, q, s):
+        enters = (chip > 0) if side == 0 else (chip < n_chips - 1)
+        rows = sub_rows(q, s)
+
+        @pl.when((chip < q) if side == 0 else (chip > q))
+        def _():
+            @pl.when(enters)
+            def _():
+                rs_copy(side, q, s).wait_recv()
+                w_part[rows, :] += rs_in[side, in_rows(q, s), :]
+
+            rs_copy(side, q, s).start()
+
+    def spread(q, s):
+        @pl.when(chip != q)
+        def _():
+            ag_copy(0, q, s).wait_recv()
+
+        @pl.when((chip >= q) & (chip < n_chips - 1))
+        def _():
+            ag_copy(0, q, s).start()
+
+        @pl.when((chip <= q) & (chip > 0))
+        def _():
+            ag_copy(1, q, s).start()
+
+        ag_copy(2, q, s).start()
+
+    w_part[half_rows(core), :] += w_in[...]
+
+    @pl.loop(0, SUBS)
+    def _(s):
+        for k in range(n_chips - 1):
+            flow(0, n_chips - 1 - k, s)
+            flow(1, k, s)
+        mine = chip
+        rows = sub_rows(mine, s)
+
+        @pl.when(chip > 0)
+        def _():
+            rs_copy(0, mine, s).wait_recv()
+            w_part[rows, :] += rs_in[0, in_rows(mine, s), :]
+
+        @pl.when(chip < n_chips - 1)
+        def _():
+            rs_copy(1, mine, s).wait_recv()
+            w_part[rows, :] += rs_in[1, in_rows(mine, s), :]
+
+        w_out[rows, :] = w_part[rows, :]
+        spread(mine, s)
+
+        @pl.when(s > 0)
+        def _():
+            for d in range(1, n_chips):
+                spread((chip + d) % n_chips, s - 1)
+
+    for d in range(1, n_chips):
+        spread((chip + d) % n_chips, SUBS - 1)
+
+    pair.wait_send()
+
+    @pl.loop(0, SUBS)
+    def _(s):
+        for q in range(n_chips):
+            for side in range(2):
+                @pl.when((chip < q) if side == 0 else (chip > q))
+                def _():
+                    rs_copy(side, q, s).wait_send()
+
+            @pl.when((chip >= q) & (chip < n_chips - 1))
+            def _():
+                ag_copy(0, q, s).wait_send()
+
+            @pl.when((chip <= q) & (chip > 0))
+            def _():
+                ag_copy(1, q, s).wait_send()
+
+            ag_copy(2, q, s).wait_send()
+
+    other = w_out.at[half_rows(1 - core), :]
+    pltpu.make_async_copy(other, other, agp_recv).wait()
+
+    @pl.when(active)
+    def _():
+        @pl.loop(0, n_steps)
+        def _(c):
+            for a in arrays:
+                part_copy(a, c, 1 - core).wait_send()
+                finish(*red_copy(a, c))
+
         for d in range(n_dev):
             finish(*bias_copy(d))
 
@@ -347,36 +520,45 @@
     pltpu.make_async_copy(g_out, g_out, g_recv).wait()
 
 
-def group_call(xs, rels, bias, n_dev):
+def group_call(xs, rel_table, w_rel, bias, n_dev):
     n_arr, n_heads, block, dim = xs.shape
+    model = rel_table.shape[1]
     seq = block * n_dev
     n_chips = n_dev // 2
     n_tiles = seq // ROWS // 2
+    n_steps = seq // COLS
     anyw = pl.BlockSpec(memory_space=pl.ANY)
     vmem = pl.BlockSpec(memory_space=pltpu.VMEM)
     dma = pltpu.SemaphoreType.DMA
     return pl.pallas_call(
         group_kernel,
         name='rel_attention',
-        in_specs=[anyw, vmem, vmem],
-        out_specs=[anyw, anyw, vmem],
+        in_specs=[anyw, anyw, anyw, vmem],
+        out_specs=[anyw, anyw, vmem, vmem],
         out_shape=[
             jax.ShapeDtypeStruct((2, n_heads, block, dim), BF16),
-            jax.ShapeDtypeStruct((3, n_heads, dim, block), BF16),
+            jax.ShapeDtypeStruct((2, n_heads, dim, block), BF16),
             jax.ShapeDtypeStruct((n_heads, 8, dim), F32),
+            jax.ShapeDtypeStruct((model, n_heads * dim), F32),
         ],
         scratch_shapes=[
             pltpu.VMEM((n_arr, seq, dim), BF16),
             pltpu.VMEM((seq + COLS, dim), BF16),
             pltpu.VMEM((n_heads, block, dim), BF16),
+            pltpu.VMEM((block, model), BF16),
+            pltpu.VMEM((model, n_heads * dim), BF16),
             pltpu.VMEM((dim, seq), F32),
             pltpu.VMEM((dim, seq), F32),
             pltpu.VMEM((dim, seq + COLS), F32),
-            pltpu.VMEM((3, n_chips, dim, block), F32),
-            pltpu.VMEM((3, n_chips, dim, block), BF16),
+            pltpu.VMEM((3, n_steps, dim, 256), F32),
+            pltpu.VMEM((3, n_steps, dim, 256), BF16),
             pltpu.VMEM((2, seq // 2, dim), BF16),
             pltpu.VMEM((8, dim), F32),
             pltpu.VMEM((2 * n_heads, 8, dim), F32),
+            pltpu.VMEM((n_heads, dim, block), BF16),
+            pltpu.VMEM((model, n_heads * dim), F32),
+            pltpu.VMEM((model // 2, n_heads * dim), F32),
+            pltpu.VMEM((2, model // 2, n_heads * dim), F32),
             pltpu.VMEM((ROWS, seq + ROWS + COLS), F32),
             pltpu.VMEM((ROWS, 128), F32),
             pltpu.VMEM((ROWS, 128), F32),
@@ -384,10 +566,11 @@
             pltpu.VMEM((ROWS, dim), F32),
             pltpu.VMEM((ROWS, dim), F32),
             dma((n_heads, 2)), dma((n_chips, 2)), dma((n_chips, 2)), dma((n_chips, 2)),
-            dma((3, n_chips)), dma((3, n_chips)), dma((n_tiles, ROWS // 256)), dma((3, n_chips)), dma((n_dev,)), dma, dma, dma,
+            dma((3, n_steps)), dma((3, n_steps)), dma((n_tiles, ROWS // 256)), dma((3, n_steps)), dma((n_dev,)), dma, dma, dma, dma((2,)),
+            dma, dma, dma, dma((2, n_chips, SUBS)), dma((2, n_chips, SUBS)), dma((3, n_chips, SUBS)), dma((n_chips, SUBS)), dma,
         ],
-        compiler_params=pltpu.CompilerParams(vmem_limit_bytes=63 * 2**20, collective_id=0, has_side_effects=True),
-    )(xs, rels, bias)
+        compiler_params=pltpu.CompilerParams(vmem_limit_bytes=67043328, collective_id=0, has_side_effects=True),
+    )(xs, rel_table, w_rel, bias)
 
 
 def solution(mesh):
@@ -398,12 +581,9 @@
 
     def local_fn(q, k, v, u_bias, v_bias, rel_table, w_rel, d_out):
         block, n_heads, dim = q.shape
-        rel = jnp.einsum('uo,ojf->juf', rel_table, w_rel, preferred_element_type=F32).astype(BF16)
         xs = jnp.stack([x.transpose(1, 0, 2) for x in (q, k, v, d_out)])
         bias = jnp.pad(jnp.stack([u_bias, v_bias], axis=1), ((0, 0), (0, 6), (0, 0)))
-        o, g, d_bias = group_call(xs, rel, bias, n_dev)
-        d_rel = g[2][:, :, ::-1]
-        d_w_rel = lax.psum(jnp.einsum('uo,jfu->ojf', rel_table, d_rel, preferred_element_type=F32), 'cp')
+        o, g, d_bias, d_w = group_call(xs, rel_table, w_rel.reshape(-1, n_heads * dim), bias, n_dev)
         return (
             o[0].transpose(1, 0, 2),
             o[1].transpose(1, 0, 2),
@@ -411,7 +591,7 @@
             g[1].transpose(2, 0, 1),
             d_bias[:, 0],
             d_bias[:, 1],
-            d_w_rel,
+            d_w.reshape(-1, n_heads, dim),
         )
 
     return jax.shard_map(

time: 324 us -> 324 us (level)
  Pallas kernels: 206 us -> 306 us
  waiting for transfers between devices: 80.4 us -> 0 us
  between operations: 14.1 us -> 0.69 us
  matrix products: 8.48 us -> 0 us
    pallas_call x1, Pallas kernels: 206 us -> 306 us  [group_call(): pl.pallas_call(group_kernel, name='rel_attention', in_specs=[anyw, anyw,...]
    psum x1 -> x0, waiting for transfers between devices: 80.4 us -> none  [local_fn(): lax.psum(jnp.einsum('uo,jfu->ojf', rel_table, d_rel, preferred_element_ty...]
    dot_general x2 -> x0, matrix products: 8.48 us -> none  [the longest x1 4.33 us: local_fn(): jnp.einsum('uo,ojf->juf', rel_table, w_rel, preferred_element_type=F32)]
  transfers between devices with their start and end apart: 1 -> 0, of which waited for: 1 -> 0; matrix products, arithmetic and copies ran while one was open for 1% -> 0% of each run, Pallas kernels for 0% -> 0%
where the time goes in v3:
time: 324 us; the launch traced here: 323 us
  Pallas kernels  306 us (94%)
  local copies, waits for them, and re-layouts  14.5 us (4%)
    pallas_call x1, Pallas kernels, group_call(): pl.pallas_call(group_kernel, name='rel_attention', in_specs=[anyw, anyw,...  306 us

profile of v3, /device:TPU:0, one launch (start us, length us, event | category | flops | bytes accessed | tf_op | source)
XLA Modules:
  0.0 323.0 jit_solution(12546918723204521634)
XLA Ops:
  0.6 0.7 stack.29
  1.3 0.7 stack.30
  2.0 0.6 select_maximum_fusion.bias_ref
  2.6 0.0 copy-start.1
  2.6 0.0 copy-start.2
  2.6 0.0 copy-start.3
  2.6 0.0 copy-start.4
  2.6 1.7 copy.19
  4.4 1.4 copy.20.w_hbm
  5.8 0.0 copy-done.1
  5.8 0.0 copy-done.2
  5.8 0.0 copy-done.3
  5.8 0.0 copy-done.4
  5.8 1.7 pad_maximum_fusion.xs
  7.5 305.5 %rel_attention.1 = (bf16[2,3,768,128]{3,2,1,0:T(8,128)(2,1)}, bf16[2,3,128,768]{3,2,1,0:T(8,128)(2,1)}, f32[3,8,128]{2,1,0:T(8,128)}, f32[1536,384]{1,0:T(8,128)}) custom-call(bf16[4,3,768,128]{3,2,1,0:T(8,128)(2,1)} %pad_maximum_fusion.xs, bf16[768,1536]{1,0:T(8,128)(2,1)} %rt_hbm.1, bf16[1536,384]{1,0:T(8,128)(2,1)} %copy.20.w_hbm, ...), custom_call_target="tpu_custom_call" | custom-call | tf_op jit(solution)/shard_map/rel_attention/pallas_call | solution.py:533
  313.0 0.0 copy-start
  313.0 2.4 slice_bitcast_fusion.2
  315.4 0.8 fusion
  316.2 0.6 copy_bitcast_fusion
  316.8 0.0 copy-done
  316.8 0.1 slice_bitcast_fusion
  316.9 1.1 copy.23
  317.9 1.1 copy.22
  319.0 2.0 copy.21
  321.0 2.0 copy.24
Async XLA Ops:
  2.6 3.2 copy-start.1
  2.6 3.2 copy-start.2
  2.6 3.2 copy-start.3
  2.6 3.2 copy-start.4
  313.0 3.8 %copy-start = (bf16[2,3,128,768]{3,2,1,0:T(8,128)(2,1)S(1)}, bf16[2,3,128,768]{3,2,1,0:T(8,128)(2,1)}, u32[]{:S(2)}) copy-start(bf16[2,3,128,768]{3,2,1,0:T(8,128)(2,1)} %get-tuple-element.12) | copy-start | bytes 3538948

commit v4 on v3

--- a/solution.py
+++ b/solution.py
@@ -39,7 +39,7 @@
     return jnp.concatenate([mm(anti, x[g * 256:(g + 1) * 256]) for g in reversed(range(x.shape[0] // 256))], axis=0)
 
 
-def tile_grads(q0, out_row, q_ref, k_ref, v_ref, do_ref, rel_ref, bias_ref, o_ref, dq_ref, dkt, dvt, drt, bias_acc, buf, m_ref, l_ref, acc_ref, gu_ref, gv_ref, after_step=None):
+def tile_grads(q0, out_row, q_ref, k_ref, v_ref, do_ref, rel_ref, u_ref, vb_ref, o_ref, dq_ref, dkt, dvt, drt, bias_acc, buf, m_ref, l_ref, acc_ref, gu_ref, gv_ref, after_step=None):
     seq, dim = k_ref.shape
     scale = dim ** -0.5
     steps = (q0 + ROWS + COLS - 1) // COLS
@@ -49,8 +49,8 @@
         return pl.ds(pl.multiple_of(base, 256), size)
 
     q_wide = q_ref[at(q0, ROWS), :].astype(F32)
-    q_u = (q_wide + bias_ref[0:1, :]).astype(BF16)
-    q_v = (q_wide + bias_ref[1:2, :]).astype(BF16)
+    q_u = (q_wide + u_ref[...]).astype(BF16)
+    q_v = (q_wide + vb_ref[...]).astype(BF16)
 
     def offset_scores(c):
         buf[:, at(c * COLS + ROWS, COLS)] = mm(q_v, rel_ref[at(rel0 + c * COLS, COLS), :], NT)
@@ -146,11 +146,12 @@
     return 4 * (i // 2) + jnp.where(i % 2 == 0, core, 3 - core)
 
 
-def group_kernel(xs, rt_hbm, w_hbm, bias_ref, o_out, g_out, bias_out, w_out, xh, relh, rel_flip, rt, w2, dkt, dvt, drt, part, red, o_tiles, bias_acc, bias_in, dr_in, w_part, w_in, rs_in, *rest):
+def group_kernel(q_hbm, k_hbm, v_hbm, do_hbm, rt_hbm, w_hbm, u_ref, vb_ref, o_out, dq_out, dk_out, dv_out, du_out, dvb_out, w_out, xh, relh, rel_flip, rt, w2, dkt, dvt, drt, part, red, red_r, o_tiles, bias_acc, bias_in, dr_in, w_part, w_in, rs_in, *rest):
     scratch, sems = rest[:6], rest[6:]
     (in_send, in_recv, fwd_send, fwd_recv, part_send, part_recv, tile_send, red_send, bias_send, out_recv, g_recv, bias_recv, load_sem,
      dr_recv, pair_send, pair_recv, rs_send, rs_recv, ag_send, ag_recv, agp_recv) = sems
-    n_arr, n_heads, block, dim = xs.shape
+    inputs = (q_hbm, k_hbm, v_hbm, do_hbm)
+    n_heads, block, dim = q_hbm.shape
     n_dev = lax.axis_size('cp')
     n_chips = n_dev // 2
     seq = block * n_dev
@@ -164,9 +165,10 @@
     n_tiles = seq // ROWS // 2
 
     load_rt = pltpu.make_async_copy(rt_hbm, rt, load_sem.at[0])
-    load_w = pltpu.make_async_copy(w_hbm, w2, load_sem.at[1])
+    loads_w = [pltpu.make_async_copy(w_hbm.at[h], w2.at[:, h * dim:(h + 1) * dim], load_sem.at[1 + h]) for h in range(n_heads)]
     load_rt.start()
-    load_w.start()
+    for load_w in loads_w:
+        load_w.start()
 
     barrier = pltpu.get_barrier_semaphore()
     for d in range(1, n_dev):
@@ -182,29 +184,29 @@
     def flip_rows_of(dev):
         return pl.ds(pl.multiple_of(seq - block - dev * block, block), block)
 
-    def x_copy(dest, src_dev, src, send, recv, dev):
-        return push(src, xh.at[:, rows_of(src_dev), :], send.at[0], recv.at[0], dev)
-
-    def rel_copy(dest, src_dev, src, send, recv, dev):
+    def x_copies(src_dev, srcs, send, recv, dev):
+        return [push(srcs[a], xh.at[a, rows_of(src_dev), :], send.at[0], recv.at[0], dev) for a in range(4)]
+
+    def x_all(src_dev, send, recv):
+        rows = xh.at[:, rows_of(src_dev), :]
+        return push(rows, rows, send.at[0], recv.at[0], partner)
+
+    def rel_copy(src_dev, src, send, recv, dev):
         return push(src, relh.at[flip_rows_of(src_dev), :], send.at[1], recv.at[1], dev)
 
-    def to_head(make, srcs, dest):
-        return make(dest, me, srcs, in_send.at[dest], in_recv.at[chip], 2 * dest + core)
-
     def x_to_head(dest):
-        return to_head(x_copy, xs.at[:, dest], dest)
+        for copy in x_copies(me, [x.at[dest] for x in inputs], in_send.at[dest], in_recv.at[chip], 2 * dest + core):
+            copy.start()
 
     def rel_to_head(dest):
-        return to_head(rel_copy, rel_flip.at[dest], dest)
-
-    def x_to_partner(dev, src, recv_dev):
-        return x_copy(head, dev, src, fwd_send.at[dev // 2], fwd_recv.at[dev // 2], recv_dev)
-
-    def rel_to_partner(dev, src, recv_dev):
-        return rel_copy(head, dev, src, fwd_send.at[dev // 2], fwd_recv.at[dev // 2], recv_dev)
-
-    def x_local():
-        return pltpu.make_async_copy(xs.at[:, head], xh.at[:, rows_of(me), :], in_recv.at[chip, 0])
+        return rel_copy(me, rel_flip.at[dest], in_send.at[dest], in_recv.at[chip], 2 * dest + core)
+
+    def x_to_partner(dev, srcs):
+        for copy in x_copies(dev, srcs, fwd_send.at[dev // 2], fwd_recv.at[dev // 2], partner):
+            copy.start()
+
+    def rel_to_partner(dev, src):
+        return rel_copy(dev, src, fwd_send.at[dev // 2], fwd_recv.at[dev // 2], partner)
 
     def rel_local():
         return pltpu.make_async_copy(rel_flip.at[head], relh.at[flip_rows_of(me), :], in_recv.at[chip, 1])
@@ -216,15 +218,17 @@
         def _():
             for dest in order:
                 if dest != z:
-                    x_to_head(dest).start()
+                    x_to_head(dest)
 
     @pl.when(active)
     def _():
-        x_local().start()
-        x_to_partner(me, xs.at[:, head], partner).start()
+        for a, x in enumerate(inputs):
+            pltpu.make_async_copy(x.at[head], xh.at[a, rows_of(me), :], in_recv.at[chip, 0]).start()
+        x_to_partner(me, [x.at[head] for x in inputs])
 
     load_rt.wait()
-    load_w.wait()
+    for load_w in loads_w:
+        load_w.wait()
     n_groups = block // 256
 
     @pl.loop(0, n_groups)
@@ -245,7 +249,7 @@
     @pl.when(active)
     def _():
         rel_local().start()
-        rel_to_partner(me, rel_flip.at[head], partner).start()
+        rel_to_partner(me, rel_flip.at[head]).start()
 
     dkt[...] = jnp.zeros_like(dkt)
     dvt[...] = jnp.zeros_like(dvt)
@@ -276,12 +280,12 @@
     def piece_of(g):
         return pl.ds(pl.multiple_of(g * 256, 256), 256)
 
-    def tile_copy(i, g):
+    def tile_copy(i, g, a):
         piece = tile_index(i, core) * pieces + g
         owner = piece // per
-        src = o_tiles.at[:, piece_of(i * pieces + g), :]
-        dst = o_out.at[:, head, piece_of(piece % per), :]
-        return owner, lambda: pltpu.make_async_copy(src, dst, out_recv), lambda: push(src, dst, tile_send.at[i, g], out_recv, owner)
+        src = o_tiles.at[a, piece_of(i * pieces + g), :]
+        dst = (o_out, dq_out)[a].at[head, piece_of(piece % per), :]
+        return owner, lambda: pltpu.make_async_copy(src, dst, out_recv.at[a]), lambda: push(src, dst, tile_send.at[i, g, a], out_recv.at[a], owner)
 
     def ready_blocks(i):
         return (2 * ROWS * i + block - 1) // block
@@ -295,17 +299,19 @@
     def red_copy(a, c):
         piece = 2 * c + core
         if a == 2:
-            owner, dst, recv = n_dev - 1 - piece // per, dr_in.at[head, :, piece_of(piece % per)], dr_recv
+            src, owner, dst, recv = red_r.at[c], n_dev - 1 - piece // per, dr_in.at[head, :, piece_of(piece % per)], dr_recv
         else:
-            owner, dst, recv = piece // per, g_out.at[a, head, :, piece_of(piece % per)], g_recv
-        src = red.at[a, c]
+            src, owner, dst, recv = red.at[a, c], piece // per, (dk_out, dv_out)[a].at[head, piece_of(piece % per), :], g_recv.at[a]
         return owner, lambda: pltpu.make_async_copy(src, dst, recv), lambda: push(src, dst, red_send.at[a, c], recv, owner)
 
     def reduce(c):
         for a in arrays:
             part_copy(a, c, core).wait_recv()
             total = accs[a][:, piece_of(2 * c + core)] + part[a, c]
-            red[a, c] = (total if a == 1 else total * scale).astype(BF16)
+            if a == 2:
+                red_r[c] = (total * scale).astype(BF16)
+            else:
+                red[a, c] = (total if a == 1 else total * scale).T.astype(BF16)
             start(*red_copy(a, c))
 
     lag = 2
@@ -326,30 +332,34 @@
     @pl.when(active)
     def _():
         def tile(i, **kw):
-            @pl.loop(ready_blocks(i), ready_blocks(i + 1))
-            def _(dev):
-                @pl.when(dev == me)
-                def _():
-                    x_local().wait()
-                    rel_local().wait()
-
-                @pl.when((dev % 2 == core) & (dev != me))
-                def _():
-                    x_copy(head, dev, xs.at[:, head], in_send.at[0], in_recv.at[dev // 2], partner).wait_recv()
-                    rel_copy(head, dev, rel_flip.at[head], in_send.at[0], in_recv.at[dev // 2], partner).wait_recv()
-                    x_to_partner(dev, xh.at[:, rows_of(dev), :], partner).start()
-                    rel_to_partner(dev, relh.at[flip_rows_of(dev), :], partner).start()
-
-            @pl.loop(ready_blocks(i), ready_blocks(i + 1))
-            def _(dev):
-                @pl.when(dev % 2 != core)
-                def _():
-                    x_to_partner(dev, xs.at[:, head], partner).wait_recv()
-                    rel_to_partner(dev, rel_flip.at[head], partner).wait_recv()
-
-            tile_grads(tile_index(i, core) * ROWS, i * ROWS, q_ref, k_ref, v_ref, do_ref, relh, bias_ref.at[head], o_tiles.at[0], o_tiles.at[1], dkt, dvt, drt, bias_acc, *scratch, **kw)
+            with jax.named_scope('wait_ici'):
+                @pl.loop(ready_blocks(i), ready_blocks(i + 1))
+                def _(dev):
+                    @pl.when(dev == me)
+                    def _():
+                        local = xh.at[:, rows_of(me), :]
+                        pltpu.make_async_copy(local, local, in_recv.at[chip, 0]).wait()
+                        rel_local().wait()
+
+                    @pl.when((dev % 2 == core) & (dev != me))
+                    def _():
+                        x_all(dev, in_send.at[0], in_recv.at[dev // 2]).wait_recv()
+                        rel_copy(dev, rel_flip.at[head], in_send.at[0], in_recv.at[dev // 2], partner).wait_recv()
+                        x_to_partner(dev, [xh.at[a, rows_of(dev), :] for a in range(4)])
+                        rel_to_partner(dev, relh.at[flip_rows_of(dev), :]).start()
+
+            with jax.named_scope('wait_core'):
+                @pl.loop(ready_blocks(i), ready_blocks(i + 1))
+                def _(dev):
+                    @pl.when(dev % 2 != core)
+                    def _():
+                        x_all(dev, fwd_send.at[dev // 2], fwd_recv.at[dev // 2]).wait_recv()
+                        rel_to_partner(dev, rel_flip.at[head]).wait_recv()
+
+            tile_grads(tile_index(i, core) * ROWS, i * ROWS, q_ref, k_ref, v_ref, do_ref, relh, u_ref.at[pl.ds(head, 1), :], vb_ref.at[pl.ds(head, 1), :], o_tiles.at[0], o_tiles.at[1], dkt, dvt, drt, bias_acc, *scratch, **kw)
             for g in range(pieces):
-                start(*tile_copy(i, g))
+                for a in range(2):
+                    start(*tile_copy(i, g, a))
 
         @pl.loop(0, n_tiles - 1)
         def _(i):
@@ -364,9 +374,10 @@
         def _(c):
             reduce(c)
 
-    half, quarter = w_part.shape[0] // 2, w_part.shape[0] // 2 // n_chips
+    half, quarter = w_part.shape[1] // 2, w_part.shape[1] // 2 // n_chips
     sub = quarter // SUBS
-    pltpu.make_async_copy(dr_in, dr_in, dr_recv).wait()
+    with jax.named_scope('wait_drel'):
+        pltpu.make_async_copy(dr_in, dr_in, dr_recv).wait()
 
     def d_rel_of(h):
         return jnp.concatenate([mm(dr_in[h, :, g * 256:(g + 1) * 256], anti) for g in reversed(range(n_groups))], axis=1).astype(BF16)
@@ -380,13 +391,17 @@
         @pl.loop(0, half // 256)
         def _(g):
             rows = pl.ds(pl.multiple_of(c * half + g * 256, 256), 256)
-            w_part[rows, :] = lax.dot_general(rt[:, rows], d_rel, (((0,), (1,)), ((), ())), preferred_element_type=F32)
-
-    pair = push(w_part.at[half_rows(1 - core), :], w_in, pair_send, pair_recv, partner)
-    w_rows(1 - core)
-    pair.start()
-    w_rows(core)
-    pair.wait_recv()
+            term = lax.dot_general(rt[:, rows], d_rel, (((0,), (1,)), ((), ())), preferred_element_type=F32)
+            for h in range(n_heads):
+                w_part[h, rows, :] = term[:, h * dim:(h + 1) * dim]
+
+    pair = push(w_part.at[:, half_rows(1 - core), :], w_in, pair_send, pair_recv, partner)
+    with jax.named_scope('w_mm'):
+        w_rows(1 - core)
+        pair.start()
+        w_rows(core)
+        pair.wait_recv()
+        w_part[:, half_rows(core), :] += w_in[...]
 
     def sub_rows(q, s):
         return pl.ds(pl.multiple_of(core * half + q * quarter + s * sub, 8), sub)
@@ -395,28 +410,39 @@
         return pl.ds(pl.multiple_of(q * quarter + s * sub, 8), sub)
 
     def rs_copy(side, q, s):
-        dev = 2 * (chip + (1 if side == 0 else -1)) + core
-        dev = jnp.clip(dev, 0, n_dev - 1)
-        return push(w_part.at[sub_rows(q, s), :], rs_in.at[side, in_rows(q, s), :], rs_send.at[side, q, s], rs_recv.at[side, q, s], dev)
+        dev = jnp.clip(2 * (chip + (1 if side == 0 else -1)) + core, 0, n_dev - 1)
+        return push(w_part.at[:, sub_rows(q, s), :], rs_in.at[side, :, in_rows(q, s), :], rs_send.at[side, q, s], rs_recv.at[side, q, s], dev)
 
     def ag_copy(way, q, s):
-        dev = (2 * (chip + 1) + core, 2 * (chip - 1) + core, partner)[way]
-        dev = jnp.clip(dev, 0, n_dev - 1)
+        dev = jnp.clip((2 * (chip + 1) + core, 2 * (chip - 1) + core, partner)[way], 0, n_dev - 1)
+        rows = w_out.at[:, sub_rows(q, s), :]
+        return push(rows, rows, ag_send.at[way, q, s], agp_recv if way == 2 else ag_recv.at[q, s], dev)
+
+    def add_in(side, q, s):
+        rs_copy(side, q, s).wait_recv()
         rows = sub_rows(q, s)
-        return push(w_out.at[rows, :], w_out.at[rows, :], ag_send.at[way, q, s], agp_recv if way == 2 else ag_recv.at[q, s], dev)
+        w_part[:, rows, :] += rs_in[side, :, in_rows(q, s), :]
 
     def flow(side, q, s):
-        enters = (chip > 0) if side == 0 else (chip < n_chips - 1)
-        rows = sub_rows(q, s)
-
-        @pl.when((chip < q) if side == 0 else (chip > q))
-        def _():
-            @pl.when(enters)
-            def _():
-                rs_copy(side, q, s).wait_recv()
-                w_part[rows, :] += rs_in[side, in_rows(q, s), :]
-
+        middle = (chip > 0) & (chip < n_chips - 1)
+
+        @pl.when(middle & ((chip < q) if side == 0 else (chip > q)))
+        def _():
+            add_in(side, q, s)
             rs_copy(side, q, s).start()
+
+    def settle(s):
+        @pl.when(chip > 0)
+        def _():
+            add_in(0, chip, s)
+
+        @pl.when(chip < n_chips - 1)
+        def _():
+            add_in(1, chip, s)
+
+        rows = sub_rows(chip, s)
+        w_out[:, rows, :] = w_part[:, rows, :]
+        spread(chip, s)
 
     def spread(q, s):
         @pl.when(chip != q)
@@ -433,36 +459,29 @@
 
         ag_copy(2, q, s).start()
 
-    w_part[half_rows(core), :] += w_in[...]
-
-    @pl.loop(0, SUBS)
-    def _(s):
-        for k in range(n_chips - 1):
-            flow(0, n_chips - 1 - k, s)
-            flow(1, k, s)
-        mine = chip
-        rows = sub_rows(mine, s)
-
-        @pl.when(chip > 0)
-        def _():
-            rs_copy(0, mine, s).wait_recv()
-            w_part[rows, :] += rs_in[0, in_rows(mine, s), :]
-
-        @pl.when(chip < n_chips - 1)
-        def _():
-            rs_copy(1, mine, s).wait_recv()
-            w_part[rows, :] += rs_in[1, in_rows(mine, s), :]
-
-        w_out[rows, :] = w_part[rows, :]
-        spread(mine, s)
-
-        @pl.when(s > 0)
-        def _():
-            for d in range(1, n_chips):
-                spread((chip + d) % n_chips, s - 1)
-
-    for d in range(1, n_chips):
-        spread((chip + d) % n_chips, SUBS - 1)
+    with jax.named_scope('rs_ag'):
+        @pl.when(chip == 0)
+        def _():
+            for s in range(SUBS):
+                for q in reversed(range(1, n_chips)):
+                    rs_copy(0, q, s).start()
+
+        @pl.when(chip == n_chips - 1)
+        def _():
+            for s in range(SUBS):
+                for q in range(n_chips - 1):
+                    rs_copy(1, q, s).start()
+
+        for s in range(SUBS + 2):
+            if s < SUBS:
+                for k in range(n_chips - 1):
+                    flow(0, n_chips - 1 - k, s)
+                    flow(1, k, s)
+            if 1 <= s <= SUBS:
+                settle(s - 1)
+            if s >= 2:
+                for d in range(1, n_chips):
+                    spread((chip + d) % n_chips, s - 2)
 
     pair.wait_send()
 
@@ -484,7 +503,7 @@
 
             ag_copy(2, q, s).wait_send()
 
-    other = w_out.at[half_rows(1 - core), :]
+    other = w_out.at[:, half_rows(1 - core), :]
     pltpu.make_async_copy(other, other, agp_recv).wait()
 
     @pl.when(active)
@@ -501,27 +520,35 @@
         @pl.loop(0, n_tiles)
         def _(i):
             for g in range(pieces):
-                finish(*tile_copy(i, g))
+                for a in range(2):
+                    finish(*tile_copy(i, g, a))
 
         @pl.loop(0, n_chips)
         def _(z):
-            x_to_partner(2 * z + core, xs.at[:, head], partner).wait_send()
-            rel_to_partner(2 * z + core, rel_flip.at[head], partner).wait_send()
+            dev = 2 * z + core
+            x_all(dev, fwd_send.at[z], fwd_recv.at[z]).wait_send()
+            rel_to_partner(dev, rel_flip.at[head]).wait_send()
 
     for dest in range(n_heads):
         @pl.when(chip != dest)
         def _():
-            x_to_head(dest).wait_send()
+            x_all(me, in_send.at[dest], in_recv.at[chip]).wait_send()
             rel_to_head(dest).wait_send()
     pltpu.make_async_copy(bias_in, bias_in, bias_recv).wait()
     for h in range(n_heads):
-        bias_out[h] = bias_in[2 * h] + bias_in[2 * h + 1]
-    pltpu.make_async_copy(o_out, o_out, out_recv).wait()
-    pltpu.make_async_copy(g_out, g_out, g_recv).wait()
-
-
-def group_call(xs, rel_table, w_rel, bias, n_dev):
-    n_arr, n_heads, block, dim = xs.shape
+        both = bias_in[2 * h] + bias_in[2 * h + 1]
+        du_out[h:h + 1, :] = both[0:1]
+        dvb_out[h:h + 1, :] = both[1:2]
+    with jax.named_scope('wait_results'):
+        for a in range(2):
+            pltpu.make_async_copy((o_out, dq_out)[a], (o_out, dq_out)[a], out_recv.at[a]).wait()
+            pltpu.make_async_copy((dk_out, dv_out)[a], (dk_out, dv_out)[a], g_recv.at[a]).wait()
+
+
+def group_call(q, k, v, d_out, rel_table, w_rel, u_bias, v_bias, n_dev):
+    n_heads, block, dim = q.shape
+    like_q = jax.ShapeDtypeStruct((n_heads, block, dim), BF16)
+    like_u = jax.ShapeDtypeStruct((n_heads, dim), F32)
     model = rel_table.shape[1]
     seq = block * n_dev
     n_chips = n_dev // 2
@@ -533,16 +560,11 @@
     return pl.pallas_call(
         group_kernel,
         name='rel_attention',
-        in_specs=[anyw, anyw, anyw, vmem],
-        out_specs=[anyw, anyw, vmem, vmem],
-        out_shape=[
-            jax.ShapeDtypeStruct((2, n_heads, block, dim), BF16),
-            jax.ShapeDtypeStruct((2, n_heads, dim, block), BF16),
-            jax.ShapeDtypeStruct((n_heads, 8, dim), F32),
-            jax.ShapeDtypeStruct((model, n_heads * dim), F32),
-        ],
+        in_specs=[anyw] * 6 + [vmem] * 2,
+        out_specs=[anyw] * 4 + [vmem] * 3,
+        out_shape=[like_q] * 4 + [like_u] * 2 + [jax.ShapeDtypeStruct((n_heads, model, dim), F32)],
         scratch_shapes=[
-            pltpu.VMEM((n_arr, seq, dim), BF16),
+            pltpu.VMEM((4, seq, dim), BF16),
             pltpu.VMEM((seq + COLS, dim), BF16),
             pltpu.VMEM((n_heads, block, dim), BF16),
             pltpu.VMEM((block, model), BF16),
@@ -551,14 +573,15 @@
             pltpu.VMEM((dim, seq), F32),
             pltpu.VMEM((dim, seq + COLS), F32),
             pltpu.VMEM((3, n_steps, dim, 256), F32),
-            pltpu.VMEM((3, n_steps, dim, 256), BF16),
+            pltpu.VMEM((2, n_steps, 256, dim), BF16),
+            pltpu.VMEM((n_steps, dim, 256), BF16),
             pltpu.VMEM((2, seq // 2, dim), BF16),
             pltpu.VMEM((8, dim), F32),
             pltpu.VMEM((2 * n_heads, 8, dim), F32),
             pltpu.VMEM((n_heads, dim, block), BF16),
-            pltpu.VMEM((model, n_heads * dim), F32),
-            pltpu.VMEM((model // 2, n_heads * dim), F32),
-            pltpu.VMEM((2, model // 2, n_heads * dim), F32),
+            pltpu.VMEM((n_heads, model, dim), F32),
+            pltpu.VMEM((n_heads, model // 2, dim), F32),
+            pltpu.VMEM((2, n_heads, model // 2, dim), F32),
             pltpu.VMEM((ROWS, seq + ROWS + COLS), F32),
             pltpu.VMEM((ROWS, 128), F32),
             pltpu.VMEM((ROWS, 128), F32),
@@ -566,11 +589,11 @@
             pltpu.VMEM((ROWS, dim), F32),
             pltpu.VMEM((ROWS, dim), F32),
             dma((n_heads, 2)), dma((n_chips, 2)), dma((n_chips, 2)), dma((n_chips, 2)),
-            dma((3, n_steps)), dma((3, n_steps)), dma((n_tiles, ROWS // 256)), dma((3, n_steps)), dma((n_dev,)), dma, dma, dma, dma((2,)),
+            dma((3, n_steps)), dma((3, n_steps)), dma((n_tiles, ROWS // 256, 2)), dma((3, n_steps)), dma((n_dev,)), dma((2,)), dma((2,)), dma, dma((1 + n_heads,)),
             dma, dma, dma, dma((2, n_chips, SUBS)), dma((2, n_chips, SUBS)), dma((3, n_chips, SUBS)), dma((n_chips, SUBS)), dma,
         ],
         compiler_params=pltpu.CompilerParams(vmem_limit_bytes=67043328, collective_id=0, has_side_effects=True),
-    )(xs, rel_table, w_rel, bias)
+    )(q, k, v, d_out, rel_table, w_rel, u_bias, v_bias)
 
 
 def solution(mesh):
@@ -580,19 +603,9 @@
     weight_spec = P(None, 'hp', None)
 
     def local_fn(q, k, v, u_bias, v_bias, rel_table, w_rel, d_out):
-        block, n_heads, dim = q.shape
-        xs = jnp.stack([x.transpose(1, 0, 2) for x in (q, k, v, d_out)])
-        bias = jnp.pad(jnp.stack([u_bias, v_bias], axis=1), ((0, 0), (0, 6), (0, 0)))
-        o, g, d_bias, d_w = group_call(xs, rel_table, w_rel.reshape(-1, n_heads * dim), bias, n_dev)
-        return (
-            o[0].transpose(1, 0, 2),
-            o[1].transpose(1, 0, 2),
-            g[0].transpose(2, 0, 1),
-            g[1].transpose(2, 0, 1),
-            d_bias[:, 0],
-            d_bias[:, 1],
-            d_w.reshape(-1, n_heads, dim),
-        )
+        swap = lambda x: x.transpose(1, 0, 2)
+        *rows, d_u, d_v, d_w = group_call(swap(q), swap(k), swap(v), swap(d_out), rel_table, swap(w_rel), u_bias, v_bias, n_dev)
+        return (*(swap(x) for x in rows), d_u, d_v, swap(d_w))
 
     return jax.shard_map(
         local_fn,

time: 324 us -> 286 us (0.88)
  Pallas kernels: 306 us -> 276 us
  local copies, waits for them, and re-layouts: 14.5 us -> 8.19 us
    pallas_call x1, Pallas kernels: 306 us -> 276 us  [group_call(): pl.pallas_call(group_kernel, name='rel_attention', in_specs=[anyw] * 6 +...]
    unnamed x15 -> x17, local copies, waits for them, and re-layouts: 6.4 us -> 8.19 us
where the time goes in v4:
time: 286 us; the launch traced here: 285 us
  Pallas kernels  276 us (97%)
  local copies, waits for them, and re-layouts  8.19 us (3%)
    pallas_call x1, Pallas kernels, group_call(): pl.pallas_call(group_kernel, name='rel_attention', in_specs=[anyw] * 6 +...  276 us
    unnamed x17, local copies, waits for them, and re-layouts  8.19 us

profile of v4, /device:TPU:0, one launch (start us, length us, event | category | flops | bytes accessed | tf_op | source)
XLA Modules:
  0.0 284.9 jit_solution(17491889148892930070)
XLA Ops:
  0.6 276.0 %rel_attention.1 = (bf16[3,768,128]{2,1,0:T(8,128)(2,1)}, bf16[3,768,128]{2,1,0:T(8,128)(2,1)}, bf16[3,768,128]{2,1,0:T(8,128)(2,1)}, bf16[3,768,128]{2,1,0:T(8,...) custom-call(bf16[3,768,128]{2,1,0:T(8,128)(2,1)} %bitcast.12, ...), custom_call_target="tpu_custom_call" | custom-call | tf_op jit(solution)/shard_map/rel_attention/pallas_call | solution.py:560
  276.6 0.0 copy-start.2
  276.6 0.0 copy-start.1
  276.7 0.0 copy-start.4
  276.7 0.0 copy-start.3
  276.7 0.0 copy-start
  276.7 2.1 copy.22
  278.8 1.9 copy.23
  280.7 0.0 copy-done.2
  280.7 0.8 copy.24
  281.5 0.0 copy-done.1
  281.5 0.8 copy.25
  282.3 0.0 copy-done.4
  282.3 0.6 copy.26
  282.9 0.0 copy-done.3
  282.9 0.6 copy.27
  283.5 0.0 copy-done
  283.5 1.4 copy.28
Async XLA Ops:
  276.6 4.0 %copy-start.2 = (bf16[3,768,128]{2,1,0:T(8,128)(2,1)S(1)}, bf16[3,768,128]{2,1,0:T(8,128)(2,1)}, u32[]{:S(2)}) copy-start(bf16[3,768,128]{2,1,0:T(8,128)(2,1)} %get-tuple-element.16) | copy-start | bytes 1769476
  276.6 4.8 %copy-start.1 = (bf16[3,768,128]{2,1,0:T(8,128)(2,1)S(1)}, bf16[3,768,128]{2,1,0:T(8,128)(2,1)}, u32[]{:S(2)}) copy-start(bf16[3,768,128]{2,1,0:T(8,128)(2,1)} %get-tuple-element.17) | copy-start | bytes 1769476
  276.7 5.7 %copy-start.4 = (f32[3,128]{1,0:T(4,128)S(1)}, f32[3,128]{1,0:T(4,128)}, u32[]{:S(2)}) copy-start(f32[3,128]{1,0:T(4,128)} %get-tuple-element.32) | copy-start | bytes 4612
  276.7 6.2 %copy-start.3 = (f32[3,128]{1,0:T(4,128)S(1)}, f32[3,128]{1,0:T(4,128)}, u32[]{:S(2)}) copy-start(f32[3,128]{1,0:T(4,128)} %get-tuple-element.33) | copy-start | bytes 4612
  276.7 6.8 %copy-start = (f32[3,1536,128]{2,1,0:T(8,128)S(1)}, f32[3,1536,128]{2,1,0:T(8,128)}, u32[]{:S(2)}) copy-start(f32[3,1536,128]{2,1,0:T(8,128)} %get-tuple-element.20) | copy-start | bytes 7077892

commit v5 on v4

--- a/solution.py
+++ b/solution.py
@@ -149,7 +149,7 @@
 def group_kernel(q_hbm, k_hbm, v_hbm, do_hbm, rt_hbm, w_hbm, u_ref, vb_ref, o_out, dq_out, dk_out, dv_out, du_out, dvb_out, w_out, xh, relh, rel_flip, rt, w2, dkt, dvt, drt, part, red, red_r, o_tiles, bias_acc, bias_in, dr_in, w_part, w_in, rs_in, *rest):
     scratch, sems = rest[:6], rest[6:]
     (in_send, in_recv, fwd_send, fwd_recv, part_send, part_recv, tile_send, red_send, bias_send, out_recv, g_recv, bias_recv, load_sem,
-     dr_recv, pair_send, pair_recv, rs_send, rs_recv, ag_send, ag_recv, agp_recv) = sems
+     dr_recv, pair_send, pair_recv, rs_send, rs_recv, ag_send, ag_recv, agp_recv, go_sem) = sems
     inputs = (q_hbm, k_hbm, v_hbm, do_hbm)
     n_heads, block, dim = q_hbm.shape
     n_dev = lax.axis_size('cp')
@@ -212,13 +212,20 @@
         return pltpu.make_async_copy(rel_flip.at[head], relh.at[flip_rows_of(me), :], in_recv.at[chip, 1])
 
     anti = (lax.broadcasted_iota(jnp.int32, (256, 256), 0) + lax.broadcasted_iota(jnp.int32, (256, 256), 1) == 255).astype(F32).astype(BF16)
-    orders = ((1, 2), (2, 0), (0, 1), (2, 0, 1))
-    for z, order in enumerate(orders):
-        @pl.when(chip == z)
-        def _():
-            for dest in order:
-                if dest != z:
-                    x_to_head(dest)
+    orders = ((1, 2), (0, 2), (1, 0), (2, 0, 1))
+
+    def first_to_head():
+        for z, order in enumerate(orders):
+            @pl.when(chip == z)
+            def _():
+                x_to_head(order[0])
+
+    def rest_to_head(z, order):
+        for dest in order[1:]:
+            x_to_head(dest)
+            rel_to_head(dest).start()
+
+    first_to_head()
 
     @pl.when(active)
     def _():
@@ -242,9 +249,9 @@
     for z, order in enumerate(orders):
         @pl.when(chip == z)
         def _():
-            for dest in order:
-                if dest != z:
-                    rel_to_head(dest).start()
+            rel_to_head(order[0]).start()
+            if z < n_chips - 1:
+                rest_to_head(z, order)
 
     @pl.when(active)
     def _():
@@ -257,6 +264,21 @@
     bias_acc[...] = jnp.zeros_like(bias_acc)
     scratch[0][:, :ROWS] = jnp.zeros((ROWS, ROWS), F32)
     relh[pl.ds(seq, COLS), :] = jnp.zeros((COLS, dim), BF16)
+
+    def sent_to_head(dest):
+        x_all(me, in_send.at[dest], in_recv.at[chip]).wait_send()
+        rel_to_head(dest).wait_send()
+
+    @pl.when(chip == n_chips - 2)
+    def _():
+        for dest in orders[n_chips - 2]:
+            sent_to_head(dest)
+        pl.semaphore_signal(go_sem, inc=1, device_id={'cp': jnp.minimum(me + 2, n_dev - 1)}, device_id_type=pl.DeviceIdType.MESH)
+
+    @pl.when(chip == n_chips - 1)
+    def _():
+        pl.semaphore_wait(go_sem, 1)
+        rest_to_head(n_chips - 1, orders[n_chips - 1])
 
     q_ref, k_ref, v_ref, do_ref = (xh.at[a] for a in range(4))
     pieces = ROWS // 256
@@ -406,102 +428,86 @@
     def sub_rows(q, s):
         return pl.ds(pl.multiple_of(core * half + q * quarter + s * sub, 8), sub)
 
-    def in_rows(q, s):
-        return pl.ds(pl.multiple_of(q * quarter + s * sub, 8), sub)
-
-    def rs_copy(side, q, s):
-        dev = jnp.clip(2 * (chip + (1 if side == 0 else -1)) + core, 0, n_dev - 1)
-        return push(w_part.at[:, sub_rows(q, s), :], rs_in.at[side, :, in_rows(q, s), :], rs_send.at[side, q, s], rs_recv.at[side, q, s], dev)
+    side = chip // 2
+    mate = chip + 1 - 2 * (chip % 2)
+    inner = (chip > 0) & (chip < n_chips - 1)
+    far_pair = 2 * (1 - side)
+    gate = 2 - side
+
+    def in_rows(s):
+        return pl.ds(pl.multiple_of(s * sub, 8), sub)
+
+    def rs_copy(q, slot, s, to):
+        return push(w_part.at[:, sub_rows(q, s), :], rs_in.at[slot, :, in_rows(s), :], rs_send.at[slot, s], rs_recv.at[slot, s], 2 * to + core)
 
     def ag_copy(way, q, s):
-        dev = jnp.clip((2 * (chip + 1) + core, 2 * (chip - 1) + core, partner)[way], 0, n_dev - 1)
         rows = w_out.at[:, sub_rows(q, s), :]
-        return push(rows, rows, ag_send.at[way, q, s], agp_recv if way == 2 else ag_recv.at[q, s], dev)
-
-    def add_in(side, q, s):
-        rs_copy(side, q, s).wait_recv()
+        return push(rows, rows, ag_send.at[way, q, s], agp_recv if way == 2 else ag_recv.at[q, s], (2 * mate + core, 2 * gate + core, partner)[way])
+
+    def add_in(q, slot, s):
+        rs_copy(q, slot, s, mate).wait_recv()
         rows = sub_rows(q, s)
-        w_part[:, rows, :] += rs_in[side, :, in_rows(q, s), :]
-
-    def flow(side, q, s):
-        middle = (chip > 0) & (chip < n_chips - 1)
-
-        @pl.when(middle & ((chip < q) if side == 0 else (chip > q)))
+        w_part[:, rows, :] += rs_in[slot, :, in_rows(s), :]
+
+    def every_part(body):
+        for s in range(SUBS):
+            body(s)
+
+    @every_part
+    def _(s):
+        @pl.when(jnp.logical_not(inner))
         def _():
-            add_in(side, q, s)
-            rs_copy(side, q, s).start()
-
-    def settle(s):
-        @pl.when(chip > 0)
-        def _():
-            add_in(0, chip, s)
-
-        @pl.when(chip < n_chips - 1)
-        def _():
-            add_in(1, chip, s)
-
+            for f in range(2):
+                rs_copy(far_pair + f, 2 + f, s, mate).start()
+
+        rs_copy(mate, 0, s, mate).start()
+
+    @pl.when(inner)
+    def _():
+        @every_part
+        def _(s):
+            for f in range(2):
+                add_in(far_pair + f, 2 + f, s)
+                push(w_part.at[:, sub_rows(far_pair + f, s), :], rs_in.at[1, :, in_rows(s), :], rs_send.at[2 + f, s], rs_recv.at[1, s], 2 * (far_pair + f) + core).start()
+
+    @every_part
+    def _(s):
+        add_in(chip, 0, s)
+        add_in(chip, 1, s)
         rows = sub_rows(chip, s)
         w_out[:, rows, :] = w_part[:, rows, :]
-        spread(chip, s)
-
-    def spread(q, s):
-        @pl.when(chip != q)
-        def _():
-            ag_copy(0, q, s).wait_recv()
-
-        @pl.when((chip >= q) & (chip < n_chips - 1))
-        def _():
-            ag_copy(0, q, s).start()
-
-        @pl.when((chip <= q) & (chip > 0))
-        def _():
-            ag_copy(1, q, s).start()
-
-        ag_copy(2, q, s).start()
-
-    with jax.named_scope('rs_ag'):
-        @pl.when(chip == 0)
-        def _():
-            for s in range(SUBS):
-                for q in reversed(range(1, n_chips)):
-                    rs_copy(0, q, s).start()
-
-        @pl.when(chip == n_chips - 1)
-        def _():
-            for s in range(SUBS):
-                for q in range(n_chips - 1):
-                    rs_copy(1, q, s).start()
-
-        for s in range(SUBS + 2):
-            if s < SUBS:
-                for k in range(n_chips - 1):
-                    flow(0, n_chips - 1 - k, s)
-                    flow(1, k, s)
-            if 1 <= s <= SUBS:
-                settle(s - 1)
-            if s >= 2:
-                for d in range(1, n_chips):
-                    spread((chip + d) % n_chips, s - 2)
+        for way in range(3):
+            ag_copy(way, chip, s).start()
+
+    @every_part
+    def _(s):
+        ag_copy(0, mate, s).wait_recv()
+        ag_copy(2, mate, s).start()
+        for f in range(2):
+            ag_copy(0, far_pair + f, s).wait_recv()
+
+            @pl.when(inner)
+            def _():
+                ag_copy(0, far_pair + f, s).start()
+
+            ag_copy(2, far_pair + f, s).start()
 
     pair.wait_send()
 
     @pl.loop(0, SUBS)
     def _(s):
-        for q in range(n_chips):
-            for side in range(2):
-                @pl.when((chip < q) if side == 0 else (chip > q))
-                def _():
-                    rs_copy(side, q, s).wait_send()
-
-            @pl.when((chip >= q) & (chip < n_chips - 1))
+        rs_copy(mate, 0, s, mate).wait_send()
+        for f in range(2):
+            rs_copy(far_pair + f, 2 + f, s, mate).wait_send()
+
+            @pl.when(inner)
             def _():
-                ag_copy(0, q, s).wait_send()
-
-            @pl.when((chip <= q) & (chip > 0))
-            def _():
-                ag_copy(1, q, s).wait_send()
-
-            ag_copy(2, q, s).wait_send()
+                ag_copy(0, far_pair + f, s).wait_send()
+
+            ag_copy(2, far_pair + f, s).wait_send()
+        ag_copy(2, mate, s).wait_send()
+        for way in range(3):
+            ag_copy(way, chip, s).wait_send()
 
     other = w_out.at[:, half_rows(1 - core), :]
     pltpu.make_async_copy(other, other, agp_recv).wait()
@@ -530,10 +536,9 @@
             rel_to_partner(dev, rel_flip.at[head]).wait_send()
 
     for dest in range(n_heads):
-        @pl.when(chip != dest)
+        @pl.when((chip != dest) & (chip != n_chips - 2))
         def _():
-            x_all(me, in_send.at[dest], in_recv.at[chip]).wait_send()
-            rel_to_head(dest).wait_send()
+            sent_to_head(dest)
     pltpu.make_async_copy(bias_in, bias_in, bias_recv).wait()
     for h in range(n_heads):
         both = bias_in[2 * h] + bias_in[2 * h + 1]
@@ -581,7 +586,7 @@
             pltpu.VMEM((n_heads, dim, block), BF16),
             pltpu.VMEM((n_heads, model, dim), F32),
             pltpu.VMEM((n_heads, model // 2, dim), F32),
-            pltpu.VMEM((2, n_heads, model // 2, dim), F32),
+            pltpu.VMEM((4, n_heads, model // 2 // n_chips, dim), F32),
             pltpu.VMEM((ROWS, seq + ROWS + COLS), F32),
             pltpu.VMEM((ROWS, 128), F32),
             pltpu.VMEM((ROWS, 128), F32),
@@ -590,7 +595,7 @@
             pltpu.VMEM((ROWS, dim), F32),
             dma((n_heads, 2)), dma((n_chips, 2)), dma((n_chips, 2)), dma((n_chips, 2)),
             dma((3, n_steps)), dma((3, n_steps)), dma((n_tiles, ROWS // 256, 2)), dma((3, n_steps)), dma((n_dev,)), dma((2,)), dma((2,)), dma, dma((1 + n_heads,)),
-            dma, dma, dma, dma((2, n_chips, SUBS)), dma((2, n_chips, SUBS)), dma((3, n_chips, SUBS)), dma((n_chips, SUBS)), dma,
+            dma, dma, dma, dma((4, SUBS)), dma((4, SUBS)), dma((3, n_chips, SUBS)), dma((n_chips, SUBS)), dma, pltpu.SemaphoreType.REGULAR,
         ],
         compiler_params=pltpu.CompilerParams(vmem_limit_bytes=67043328, collective_id=0, has_side_effects=True),
     )(q, k, v, d_out, rel_table, w_rel, u_bias, v_bias)

time: 286 us -> 237 us (0.83)
  Pallas kernels: 276 us -> 226 us
    pallas_call x1, Pallas kernels: 276 us -> 226 us  [group_call(): pl.pallas_call(group_kernel, name='rel_attention', in_specs=[anyw] * 6 +...]
where the time goes in v5:
time: 237 us; the launch traced here: 235 us
  Pallas kernels  226 us (95%)
  local copies, waits for them, and re-layouts  8.19 us (3%)
    pallas_call x1, Pallas kernels, group_call(): pl.pallas_call(group_kernel, name='rel_attention', in_specs=[anyw] * 6 +...  226 us
    unnamed x17, local copies, waits for them, and re-layouts  8.19 us

profile of v5, /device:TPU:0, one launch (start us, length us, event | category | flops | bytes accessed | tf_op | source)
XLA Modules:
  0.0 234.9 jit_solution(6882397061733469079)
XLA Ops:
  0.6 226.1 %rel_attention.1 = (bf16[3,768,128]{2,1,0:T(8,128)(2,1)}, bf16[3,768,128]{2,1,0:T(8,128)(2,1)}, bf16[3,768,128]{2,1,0:T(8,128)(2,1)}, bf16[3,768,128]{2,1,0:T(8,...) custom-call(bf16[3,768,128]{2,1,0:T(8,128)(2,1)} %bitcast.12, ...), custom_call_target="tpu_custom_call" | custom-call | tf_op jit(solution)/shard_map/rel_attention/pallas_call | solution.py:565
  226.7 0.0 copy-start.2
  226.7 0.0 copy-start.1
  226.7 0.0 copy-start.4
  226.7 0.0 copy-start.3
  226.7 0.0 copy-start
  226.7 2.1 copy.22
  228.8 1.9 copy.23
  230.7 0.0 copy-done.2
  230.7 0.8 copy.24
  231.5 0.0 copy-done.1
  231.5 0.8 copy.25
  232.4 0.0 copy-done.4
  232.4 0.6 copy.26
  232.9 0.0 copy-done.3
  232.9 0.6 copy.27
  233.5 0.0 copy-done
  233.5 1.4 copy.28
Async XLA Ops:
  226.7 4.0 %copy-start.2 = (bf16[3,768,128]{2,1,0:T(8,128)(2,1)S(1)}, bf16[3,768,128]{2,1,0:T(8,128)(2,1)}, u32[]{:S(2)}) copy-start(bf16[3,768,128]{2,1,0:T(8,128)(2,1)} %get-tuple-element.16) | copy-start | bytes 1769476
  226.7 4.8 %copy-start.1 = (bf16[3,768,128]{2,1,0:T(8,128)(2,1)S(1)}, bf16[3,768,128]{2,1,0:T(8,128)(2,1)}, u32[]{:S(2)}) copy-start(bf16[3,768,128]{2,1,0:T(8,128)(2,1)} %get-tuple-element.17) | copy-start | bytes 1769476
  226.7 5.7 %copy-start.4 = (f32[3,128]{1,0:T(4,128)S(1)}, f32[3,128]{1,0:T(4,128)}, u32[]{:S(2)}) copy-start(f32[3,128]{1,0:T(4,128)} %get-tuple-element.32) | copy-start | bytes 4612
  226.7 6.2 %copy-start.3 = (f32[3,128]{1,0:T(4,128)S(1)}, f32[3,128]{1,0:T(4,128)}, u32[]{:S(2)}) copy-start(f32[3,128]{1,0:T(4,128)} %get-tuple-element.33) | copy-start | bytes 4612
  226.7 6.8 %copy-start = (f32[3,1536,128]{2,1,0:T(8,128)S(1)}, f32[3,1536,128]{2,1,0:T(8,128)}, u32[]{:S(2)}) copy-start(f32[3,1536,128]{2,1,0:T(8,128)} %get-tuple-element.20) | copy-start | bytes 7077892

commit v6 on v5

--- a/solution.py
+++ b/solution.py
@@ -39,6 +39,24 @@
     return jnp.concatenate([mm(anti, x[g * 256:(g + 1) * 256]) for g in reversed(range(x.shape[0] // 256))], axis=0)
 
 
+def flip_eights(x):
+    back = 7 - lax.broadcasted_iota(jnp.int32, (8, 128), 0)
+    rows = []
+    for r in range(0, x.shape[0], 8):
+        rows.append(jnp.concatenate([jnp.take_along_axis(x[r:r + 8, c:c + 128], back, axis=0, mode='promise_in_bounds') for c in range(0, x.shape[1], 128)], axis=1))
+    return jnp.concatenate(rows, axis=0)
+
+
+def shear_back(buf, start):
+    out = []
+    for g in range(ROWS // 8):
+        left = ROWS - 8 - 8 * g
+        base = start - 128 * (left // 128 + 1)
+        part = flip_eights(buf[8 * g:8 * g + 8, pl.ds(pl.multiple_of(base, 128), COLS + 128)])
+        out.append(pltpu.roll(part, left % 128, 1, stride=1, stride_axis=0)[:, 128:])
+    return jnp.concatenate(out, axis=0)
+
+
 def tile_grads(q0, out_row, q_ref, k_ref, v_ref, do_ref, rel_ref, u_ref, vb_ref, o_ref, dq_ref, dkt, dvt, drt, bias_acc, buf, m_ref, l_ref, acc_ref, gu_ref, gv_ref, after_step=None):
     seq, dim = k_ref.shape
     scale = dim ** -0.5
@@ -65,11 +83,12 @@
 
     m_ref[...] = jnp.full_like(m_ref, -jnp.inf)
     offset_scores(0)
+    offset_scores(1)
 
     @pl.loop(0, steps - 1)
     def _(c):
-        offset_scores(c + 1)
         keep(c, scores(c))
+        offset_scores(c + 2)
 
     row_minus_col = lax.broadcasted_iota(jnp.int32, (ROWS, COLS), 0) - lax.broadcasted_iota(jnp.int32, (ROWS, COLS), 1)
     last = steps - 1
@@ -93,11 +112,9 @@
     d_out = do_ref[at(q0, ROWS), :]
     do_wide = d_out.astype(F32)
     delta = jnp.sum(do_wide * out, axis=1, keepdims=True)
-    anti = (lax.broadcasted_iota(jnp.int32, (256, 256), 0) + lax.broadcasted_iota(jnp.int32, (256, 256), 1) == 255)
-    anti_b = anti.astype(F32).astype(BF16)
     do_t = do_wide.T.astype(BF16)
     qu_t = q_u.astype(F32).T.astype(BF16)
-    qv_rt = flip_rows(anti_b, q_v).T.astype(BF16)
+    qv_rt = flip_eights(q_v.astype(F32)).T.astype(BF16)
     gu_ref[...] = jnp.zeros_like(gu_ref)
     gv_ref[...] = jnp.zeros_like(gv_ref)
 
@@ -105,15 +122,16 @@
         j0 = c * COLS
         cols = at(j0, COLS)
         prob = buf[:, at(j0 + ROWS, COLS)] * inv_sum
-        ds = (prob * (mm(d_out, v_ref[cols, :], NT) - delta)).astype(BF16)
+        ds_wide = prob * (mm(d_out, v_ref[cols, :], NT) - delta)
+        ds = ds_wide.astype(BF16)
         dvt[:, cols] += mm(do_t, prob.astype(BF16))
         dkt[:, cols] += mm(qu_t, ds)
         gu_ref[...] += mm(ds, k_ref[cols, :])
-        buf[:, at(j0 + ROWS, COLS)] = flip_rows(anti_b, ds)
+        buf[:, at(j0 + ROWS, COLS)] = ds_wide
 
     def by_offset(c):
         c0 = c * COLS
-        ds = shear(buf, c0 + ROWS, 0).astype(BF16)
+        ds = shear_back(buf, c0 + ROWS).astype(BF16)
         cols = at(rel0 + c0, COLS)
         gv_ref[...] += mm(ds, rel_ref[cols, :])
         drt[:, cols] += mm(qv_rt, ds)
@@ -135,8 +153,7 @@
 
     g_u = gu_ref[...]
     g_vr = gv_ref[...]
-    anti_f = anti.astype(F32)
-    g_v = jnp.concatenate([mm(anti_f, g_vr[g * 256:(g + 1) * 256], precision=lax.Precision.HIGHEST) for g in reversed(range(ROWS // 256))], axis=0)
+    g_v = flip_eights(g_vr)
     dq_ref[at(out_row, ROWS), :] = ((g_u + g_v) * scale).astype(BF16)
     bias_acc[0:1, :] += jnp.sum(g_u, axis=0, keepdims=True) * scale
     bias_acc[1:2, :] += jnp.sum(g_vr, axis=0, keepdims=True) * scale
@@ -212,7 +229,7 @@
         return pltpu.make_async_copy(rel_flip.at[head], relh.at[flip_rows_of(me), :], in_recv.at[chip, 1])
 
     anti = (lax.broadcasted_iota(jnp.int32, (256, 256), 0) + lax.broadcasted_iota(jnp.int32, (256, 256), 1) == 255).astype(F32).astype(BF16)
-    orders = ((1, 2), (0, 2), (1, 0), (2, 0, 1))
+    orders = ((2, 1), (0, 2), (1, 0), (2, 0, 1))
 
     def first_to_head():
         for z, order in enumerate(orders):

time: 237 us -> 232 us (0.979)
  Pallas kernels: 226 us -> 222 us
    pallas_call x1, Pallas kernels: 226 us -> 222 us  [group_call(): pl.pallas_call(group_kernel, name='rel_attention', in_specs=[anyw] * 6 +...]
where the time goes in v6:
time: 232 us; the launch traced here: 231 us
  Pallas kernels  222 us (96%)
  local copies, waits for them, and re-layouts  8.19 us (4%)
    pallas_call x1, Pallas kernels, group_call(): pl.pallas_call(group_kernel, name='rel_attention', in_specs=[anyw] * 6 +...  222 us
    unnamed x17, local copies, waits for them, and re-layouts  8.19 us

profile of v6, /device:TPU:0, one launch (start us, length us, event | category | flops | bytes accessed | tf_op | source)
XLA Modules:
  0.0 230.8 jit_solution(13353627325175797857)
XLA Ops:
  0.6 221.9 %rel_attention.1 = (bf16[3,768,128]{2,1,0:T(8,128)(2,1)}, bf16[3,768,128]{2,1,0:T(8,128)(2,1)}, bf16[3,768,128]{2,1,0:T(8,128)(2,1)}, bf16[3,768,128]{2,1,0:T(8,...) custom-call(bf16[3,768,128]{2,1,0:T(8,128)(2,1)} %bitcast.12, ...), custom_call_target="tpu_custom_call" | custom-call | tf_op jit(solution)/shard_map/rel_attention/pallas_call | solution.py:582
  222.6 0.0 copy-start.2
  222.6 0.0 copy-start.1
  222.6 0.0 copy-start.4
  222.6 0.0 copy-start.3
  222.6 0.0 copy-start
  222.6 2.1 copy.22
  224.7 1.9 copy.23
  226.6 0.0 copy-done.2
  226.6 0.8 copy.24
  227.4 0.0 copy-done.1
  227.4 0.8 copy.25
  228.2 0.0 copy-done.4
  228.2 0.6 copy.26
  228.8 0.0 copy-done.3
  228.8 0.6 copy.27
  229.4 0.0 copy-done
  229.4 1.4 copy.28
Async XLA Ops:
  222.6 4.0 %copy-start.2 = (bf16[3,768,128]{2,1,0:T(8,128)(2,1)S(1)}, bf16[3,768,128]{2,1,0:T(8,128)(2,1)}, u32[]{:S(2)}) copy-start(bf16[3,768,128]{2,1,0:T(8,128)(2,1)} %get-tuple-element.16) | copy-start | bytes 1769476
  222.6 4.8 %copy-start.1 = (bf16[3,768,128]{2,1,0:T(8,128)(2,1)S(1)}, bf16[3,768,128]{2,1,0:T(8,128)(2,1)}, u32[]{:S(2)}) copy-start(bf16[3,768,128]{2,1,0:T(8,128)(2,1)} %get-tuple-element.17) | copy-start | bytes 1769476
  222.6 5.7 %copy-start.4 = (f32[3,128]{1,0:T(4,128)S(1)}, f32[3,128]{1,0:T(4,128)}, u32[]{:S(2)}) copy-start(f32[3,128]{1,0:T(4,128)} %get-tuple-element.32) | copy-start | bytes 4612
  222.6 6.2 %copy-start.3 = (f32[3,128]{1,0:T(4,128)S(1)}, f32[3,128]{1,0:T(4,128)}, u32[]{:S(2)}) copy-start(f32[3,128]{1,0:T(4,128)} %get-tuple-element.33) | copy-start | bytes 4612
  222.6 6.8 %copy-start = (f32[3,1536,128]{2,1,0:T(8,128)S(1)}, f32[3,1536,128]{2,1,0:T(8,128)}, u32[]{:S(2)}) copy-start(f32[3,1536,128]{2,1,0:T(8,128)} %get-tuple-element.20) | copy-start | bytes 7077892

commit v7 on v6

--- a/solution.py
+++ b/solution.py
@@ -229,7 +229,7 @@
         return pltpu.make_async_copy(rel_flip.at[head], relh.at[flip_rows_of(me), :], in_recv.at[chip, 1])
 
     anti = (lax.broadcasted_iota(jnp.int32, (256, 256), 0) + lax.broadcasted_iota(jnp.int32, (256, 256), 1) == 255).astype(F32).astype(BF16)
-    orders = ((2, 1), (0, 2), (1, 0), (2, 0, 1))
+    orders = ((1, 2), (0, 2), (1, 0), (2, 0, 1))
 
     def first_to_head():
         for z, order in enumerate(orders):
@@ -294,8 +294,18 @@
 
     @pl.when(chip == n_chips - 1)
     def _():
-        pl.semaphore_wait(go_sem, 1)
-        rest_to_head(n_chips - 1, orders[n_chips - 1])
+        @pl.when(core == 0)
+        def _():
+            pl.semaphore_wait(go_sem, 1)
+            rest_to_head(n_chips - 1, orders[n_chips - 1])
+            for dest in orders[n_chips - 1]:
+                sent_to_head(dest)
+            pl.semaphore_signal(go_sem, inc=1, device_id={'cp': partner}, device_id_type=pl.DeviceIdType.MESH)
+
+        @pl.when(core == 1)
+        def _():
+            pl.semaphore_wait(go_sem, 2)
+            rest_to_head(n_chips - 1, orders[n_chips - 1])
 
     q_ref, k_ref, v_ref, do_ref = (xh.at[a] for a in range(4))
     pieces = ROWS // 256
@@ -493,12 +503,22 @@
         add_in(chip, 1, s)
         rows = sub_rows(chip, s)
         w_out[:, rows, :] = w_part[:, rows, :]
-        for way in range(3):
-            ag_copy(way, chip, s).start()
+        ag_copy(0, chip, s).start()
+
+        @pl.when(inner)
+        def _():
+            ag_copy(1, chip, s).start()
+
+        ag_copy(2, chip, s).start()
 
     @every_part
     def _(s):
         ag_copy(0, mate, s).wait_recv()
+
+        @pl.when(inner)
+        def _():
+            ag_copy(1, mate, s).start()
+
         ag_copy(2, mate, s).start()
         for f in range(2):
             ag_copy(0, far_pair + f, s).wait_recv()
@@ -523,8 +543,13 @@
 
             ag_copy(2, far_pair + f, s).wait_send()
         ag_copy(2, mate, s).wait_send()
-        for way in range(3):
-            ag_copy(way, chip, s).wait_send()
+        ag_copy(0, chip, s).wait_send()
+        ag_copy(2, chip, s).wait_send()
+
+        @pl.when(inner)
+        def _():
+            ag_copy(1, chip, s).wait_send()
+            ag_copy(1, mate, s).wait_send()
 
     other = w_out.at[:, half_rows(1 - core), :]
     pltpu.make_async_copy(other, other, agp_recv).wait()
@@ -553,7 +578,7 @@
             rel_to_partner(dev, rel_flip.at[head]).wait_send()
 
     for dest in range(n_heads):
-        @pl.when((chip != dest) & (chip != n_chips - 2))
+        @pl.when((chip != dest) & (chip != n_chips - 2) & jnp.logical_not((chip == n_chips - 1) & (core == 0)))
         def _():
             sent_to_head(dest)
     pltpu.make_async_copy(bias_in, bias_in, bias_recv).wait()
@@ -618,6 +643,35 @@
     )(q, k, v, d_out, rel_table, w_rel, u_bias, v_bias)
 
 
+def hand_over(*refs):
+    n = (len(refs) - 2) // 3
+    srcs, dsts, bufs = refs[:n], refs[n:2 * n], refs[2 * n:3 * n]
+    in_sem, out_sem = refs[3 * n:]
+    loads = [pltpu.make_async_copy(srcs[i], bufs[i], in_sem.at[i]) for i in range(n)]
+    stores = [pltpu.make_async_copy(bufs[i], dsts[i], out_sem.at[i]) for i in range(n)]
+    for load in loads:
+        load.start()
+    for load, store in zip(loads, stores):
+        load.wait()
+        store.start()
+    for store in stores:
+        store.wait()
+
+
+def hand_over_call(arrays):
+    n = len(arrays)
+    anyw = pl.BlockSpec(memory_space=pl.ANY)
+    return pl.pallas_call(
+        hand_over,
+        name='hand_over',
+        in_specs=[anyw] * n,
+        out_specs=[anyw] * n,
+        out_shape=[jax.ShapeDtypeStruct(x.shape, x.dtype) for x in arrays],
+        scratch_shapes=[pltpu.VMEM(x.shape, x.dtype) for x in arrays] + [pltpu.SemaphoreType.DMA((n,))] * 2,
+        compiler_params=pltpu.CompilerParams(vmem_limit_bytes=67043328),
+    )(*arrays)
+
+
 def solution(mesh):
     n_dev = mesh.shape['cp']
     seq_spec = P('cp', 'hp', None)
@@ -626,7 +680,7 @@
 
     def local_fn(q, k, v, u_bias, v_bias, rel_table, w_rel, d_out):
         swap = lambda x: x.transpose(1, 0, 2)
-        *rows, d_u, d_v, d_w = group_call(swap(q), swap(k), swap(v), swap(d_out), rel_table, swap(w_rel), u_bias, v_bias, n_dev)
+        *rows, d_u, d_v, d_w = hand_over_call(group_call(swap(q), swap(k), swap(v), swap(d_out), rel_table, swap(w_rel), u_bias, v_bias, n_dev))
         return (*(swap(x) for x in rows), d_u, d_v, swap(d_w))
 
     return jax.shard_map(

time: 232 us -> 221 us (0.953)
  local copies, waits for them, and re-layouts: 8.19 us -> 0 us
  Pallas kernels: 222 us -> 219 us
    unnamed x17 -> x0, local copies, waits for them, and re-layouts: 8.19 us -> none
    pallas_call x1, Pallas kernels: 222 us -> 215 us  [group_call(): pl.pallas_call(group_kernel, name='rel_attention', in_specs=[anyw] * 6 +...]
    pallas_call x0 -> x1, Pallas kernels: none -> 4.78 us  [hand_over_call(): pl.pallas_call(hand_over, name='hand_over', in_specs=[anyw] * n, out_spec...]
where the time goes in v7:
time: 221 us; the launch traced here: 220 us
  Pallas kernels  219 us (99%)
    pallas_call x1, Pallas kernels, group_call(): pl.pallas_call(group_kernel, name='rel_attention', in_specs=[anyw] * 6 +...  215 us
    pallas_call x1, Pallas kernels, hand_over_call(): pl.pallas_call(hand_over, name='hand_over', in_specs=[anyw] * n, out_spec...  4.78 us

profile of v7, /device:TPU:0, one launch (start us, length us, event | category | flops | bytes accessed | tf_op | source)
XLA Modules:
  0.0 220.0 jit_solution(5445126765381646300)
XLA Ops:
  0.6 214.5 %rel_attention.1 = (bf16[3,768,128]{2,1,0:T(8,128)(2,1)}, bf16[3,768,128]{2,1,0:T(8,128)(2,1)}, bf16[3,768,128]{2,1,0:T(8,128)(2,1)}, bf16[3,768,128]{2,1,0:T(8,...) custom-call(bf16[3,768,128]{2,1,0:T(8,128)(2,1)} %bitcast.11, ...), custom_call_target="tpu_custom_call" | custom-call | tf_op jit(solution)/shard_map/rel_attention/pallas_call | solution.py:607
  215.2 4.8 %hand_over.1 = (bf16[3,768,128]{2,1,0:T(8,128)(2,1)}, bf16[3,768,128]{2,1,0:T(8,128)(2,1)}, bf16[3,768,128]{2,1,0:T(8,128)(2,1)}, bf16[3,768,128]{2,1,0:T(8,128)...) custom-call(bf16[3,768,128]{2,1,0:T(8,128)(2,1)} %get-tuple-element.21.refs_0_, ...), custom_call_target="tpu_custom_call" | custom-call | tf_op jit(solution)/shard_map/hand_over/pallas_call | solution.py:664

commit v8 on v7

--- a/solution.py
+++ b/solution.py
@@ -11,7 +11,7 @@
 F32, BF16 = jnp.float32, jnp.bfloat16
 ROWS = 512
 COLS = 512
-SUBS = 4
+SUBS = 8
 NT = (((1,), (1,)), ((), ()))
 NN = (((1,), (0,)), ((), ()))
 

time: 221 us -> 228 us (1.032)
  Pallas kernels: 219 us -> 228 us
    pallas_call x1, Pallas kernels: 215 us -> 223 us  [group_call(): pl.pallas_call(group_kernel, name='rel_attention', in_specs=[anyw] * 6 +...]
where the time goes in v8:
time: 228 us
  Pallas kernels  228 us (100%)
    pallas_call x1, Pallas kernels, group_call(): pl.pallas_call(group_kernel, name='rel_attention', in_specs=[anyw] * 6 +...  223 us
    pallas_call x1, Pallas kernels, hand_over_call(): pl.pallas_call(hand_over, name='hand_over', in_specs=[anyw] * n, out_spec...  4.78 us

profile of v8, /device:TPU:0, one launch (start us, length us, event | category | flops | bytes accessed | tf_op | source)
XLA Modules:
  0.0 228.2 jit_solution(15410258116500087921)
XLA Ops:
  0.6 222.8 %rel_attention.1 = (bf16[3,768,128]{2,1,0:T(8,128)(2,1)}, bf16[3,768,128]{2,1,0:T(8,128)(2,1)}, bf16[3,768,128]{2,1,0:T(8,128)(2,1)}, bf16[3,768,128]{2,1,0:T(8,...) custom-call(bf16[3,768,128]{2,1,0:T(8,128)(2,1)} %bitcast.11, ...), custom_call_target="tpu_custom_call" | custom-call | tf_op jit(solution)/shard_map/rel_attention/pallas_call | solution.py:607
  223.5 4.8 %hand_over.1 = (bf16[3,768,128]{2,1,0:T(8,128)(2,1)}, bf16[3,768,128]{2,1,0:T(8,128)(2,1)}, bf16[3,768,128]{2,1,0:T(8,128)(2,1)}, bf16[3,768,128]{2,1,0:T(8,128)...) custom-call(bf16[3,768,128]{2,1,0:T(8,128)(2,1)} %get-tuple-element.21.refs_0_, ...), custom_call_target="tpu_custom_call" | custom-call | tf_op jit(solution)/shard_map/hand_over/pallas_call | solution.py:664
